TPU v7x, 32 devices: a whole 2x2x4 slice. The times are simulated.
32 devices in a mesh: grp: 2 (over y), band: 4 (over z), mem: 2 (over x), fld: 2 (over core).
Axes of the slice: x: 2, y: 2, z: 4, core: 2. Of those that a mesh axis runs over, the one named last changes fastest.
Arguments:
- surface_fields: bfloat16 [16, 8, 8, 65536], P(('grp', 'mem'), 'fld', None, 'band'), parts along dimension 0, may hold values from -8 to 8
- land_mask: int32 [65536], P('band'), may hold values from 0 to 1, as said below
- source_area: float32 [65536], P('band'), may hold values from 0.5 to 1.5
- target_area: float32 [16384], P('band'), may hold values from 0.75 to 1.25
- weight_tiles: bfloat16 [16, 128, 128], replicated, may hold values from -1 to 1
- tile_of: int32 [128, 24], P('band'), may hold values from 0 to 15
- block_of: int32 [128, 24], P('band'), may hold values from 0 to 191, as said below
- live_slots: int32 [128], P('band'), may hold values from 1 to 24, as said below
Outputs:
- regridded: float32 [16, 8, 8, 16384], P(('grp', 'mem'), 'fld', None, 'band'), parts along dimension 0
- conserved: float32 [16, 8, 8], P(('grp', 'mem'), 'fld'), parts along dimension 0
- ensemble: float32 [16, 8], P(('grp', 'fld')), parts along dimension 0
There are 2 independent parts, one for each index of `grp`. A program takes and returns all parts, laid end to end along the dimension named above; an argument that names none is the same for every part. Nothing has to cross between parts.
Inputs may be any that keep to these rules, and one draw needn't show every extreme that they name: `land_mask`: 1 marks ocean, 0 land. `block_of`: for the target block at place j (0 to 31) within its band, every entry lies in 4 * j to 4 * j + 4 + 2 * 32 - 1; values under 32 name the lower band's last blocks, values from 160 on the higher band's first blocks. `live_slots`: slots from this count on are unused.
All inputs are finite; a program needn't handle non-finite values.
Results may differ from a plain program's by a relative error of at most 0.0014.
Values may be sent and summed in bfloat16 or wider, within the bound.
No kernel may reach another device: no remote copies, remote signals or barrier semaphores. Data moves between devices by JAX's collectives and lax.ppermute only.
A program may use at most 64 MiB of HBM per device.

v0:
```python
import jax
import jax.numpy as jnp
from jax import lax
from jax.sharding import PartitionSpec as P

MEMBERS = 8
HALO_BLK = 32


def extended_2(array, sides, width):
    for axis, dim in sides:
        size, length = (lax.axis_size(axis), array.shape[dim])
        up = [(i, (i + 1) % size) for i in range(size - 1)]
        down = [(j, i) for i, j in up]
        last = lax.slice_in_dim(array, length - width, length, axis=dim)
        leading = lax.slice_in_dim(array, 0, width, axis=dim)
        before = lax.ppermute(last, axis, up)
        after = lax.ppermute(leading, axis, down)
        array = jnp.concatenate([before, array, after], axis=dim)
    return array


def slot_terms(source, slot_names, weight_tiles, bounds):
    tile_ids, picked, usable, unused = slot_names
    columns = source.shape[0]
    tile_size = source.shape[2]
    tgt_count = picked.shape[0]

    def one_slot(position, running):
        chosen = jnp.take(source, picked[:, position], axis=1)
        weights = jnp.take(weight_tiles, tile_ids[:, position], axis=0)
        weights = jnp.where(
            usable[:, position][:, None, None], weights, jnp.zeros((), weight_tiles.dtype)
        )
        return running + jnp.einsum(
            "cnb,nbd->cnd", chosen, weights, preferred_element_type=jnp.float32
        )

    start = jnp.zeros((columns, tgt_count, tile_size), jnp.float32)
    return lax.fori_loop(bounds[0], bounds[1], one_slot, start)


def band_totals(own_total, target_part, area_part):
    return lax.psum((own_total, target_part, area_part), "band")


def on_device(
    surface_fields, land_mask, source_area, target_area, weight_tiles, tile_of, block_of, live_slots
):
    members, fields, snapshots, cell_count = surface_fields.shape
    columns = members * fields * snapshots
    tile_size = weight_tiles.shape[1]
    slot_count = tile_of.shape[1]
    tgt_count = tile_of.shape[0]
    own_blocks = cell_count // tile_size
    weighted = (
        source_area * land_mask.astype(jnp.float32) * surface_fields.astype(jnp.float32)
    ).astype(jnp.bfloat16)
    flat = weighted.reshape(columns, cell_count)
    own_total = jnp.sum(flat, axis=1, dtype=jnp.float32)
    area_part = jnp.sum(target_area)
    slot_place = lax.broadcasted_iota(jnp.int32, (tgt_count, slot_count), 1)
    slot_alive = slot_place < live_slots[:, None]
    extended = extended_2(flat, (("band", 1),), HALO_BLK * tile_size)
    source = extended.reshape(columns, own_blocks + 2 * HALO_BLK, tile_size)
    work_list = [(tile_of, block_of, slot_alive, live_slots)]
    results = [slot_terms(source, listed, weight_tiles, (0, slot_count)) for listed in work_list]
    raw_sums = results[0]
    raw_sums = raw_sums.reshape(columns, tgt_count * tile_size)
    totals = band_totals(own_total, jnp.sum(raw_sums, axis=1), area_part)
    source_total, target_total, area_total = totals
    correction = (source_total - target_total) / area_total
    regridded = raw_sums / target_area[None, :] + correction[:, None]
    conserved = (source_total / area_total).reshape(members, fields, snapshots)
    ensemble = lax.psum(jnp.sum(conserved, axis=0), "mem") / MEMBERS
    return (
        regridded.reshape(members, fields, snapshots, tgt_count * tile_size),
        conserved,
        ensemble,
    )


def solution(mesh):
    placed = (
        P(("grp", "mem"), "fld", None, "band"),
        P("band"),
        P("band"),
        P("band"),
        P(),
        P("band", None),
        P("band", None),
        P("band"),
    )
    return jax.shard_map(
        on_device,
        mesh=mesh,
        in_specs=placed,
        out_specs=(
            P(("grp", "mem"), "fld", None, "band"),
            P(("grp", "mem"), "fld", None),
            P(("grp", "fld"), None),
        ),
        check_vma=False,
    )
```

profile of v0, /device:TPU:0, one launch (start us, length us, event | category | flops | bytes accessed | tf_op | source)
XLA Modules:
  0.0 303.3 jit_solution(8360894486736070716)
XLA Ops:
  1.5 3.7 %convert_reduce_fusion = (f32[4,4,8]{2,1,0:T(4,128)S(1)}, bf16[4,4,8,16384]{3,2,1,0:T(8,128)(2,1)S(1)}) fusion(bf16[4,4,8,16384]{3,2,1,0:T(8,128)(2,1)} %param.10, f32[16384]{0:T(1024)S(1)} %convert_multiply_fusion), kind=kLoop, calls=%fused_computation.23 | loop fusion | flops 10485632 | bytes 8454656 | tf_op jit(solution)/shard_map/reduce_sum | solution.py:60
  5.3 2.0 copy-done.1
  8.5 5.0 %collective-permute-start = (bf16[128,4096]{1,0:T(8,128)(2,1)}, bf16[128,4096]{1,0:T(8,128)(2,1)S(1)}, u32[]{:S(2)}, u32[]{:S(2)}) collective-permute-start(bf16[128,4096]{1,0:T(8,128)(2,1)} %get-tuple-element.191), channel_id=1, source_target_pairs={{0,4},{4,8},{8,12},{1,5},{5,9},{9,13},{2,6},{6,10},{10,14},{3,7},{... | collective-permute-start | bytes 3145736 | tf_op jit(solution)/shard_map/ppermute | solution.py:17
  13.5 1.3 collective-permute-start.1
  15.5 20.6 %collective-permute-done = bf16[128,4096]{1,0:T(8,128)(2,1)S(1)} collective-permute-done((bf16[128,4096]{1,0:T(8,128)(2,1)}, bf16[128,4096]{1,0:T(8,128)(2,1)S(1)}, u32[]{:S(2)}, u32[]{:S(2)}) %collective-permute-start) | collective-permute-done | bytes 1048608 | tf_op jit(solution)/shard_map/ppermute | solution.py:17
  36.1 3.9 %collective-permute-done.1 = bf16[128,4096]{1,0:T(8,128)(2,1)S(1)} collective-permute-done((bf16[128,4096]{1,0:T(8,128)(2,1)S(1)}, bf16[128,4096]{1,0:T(8,128)(2,1)S(1)}, u32[]{:S(2)}, u32[]{:S(2)}) %collective-permute-start.1) | collective-permute-done | bytes 1048608 | tf_op jit(solution)/shard_map/ppermute | solution.py:18
  40.0 6.8 %pad_maximum_fusion = bf16[128,24576]{1,0:T(8,128)(2,1)} fusion(bf16[128,4096]{1,0:T(8,128)(2,1)S(1)} %collective-permute-done.1, bf16[128,16384]{1,0:T(8,128)(2,1)} %bitcast.28, bf16[128,4096]{1,0:T(8,128)(2,1)S(1)} %collective-permute-done), kind=kLoop, calls=%fused_computation.25 | loop fusion | flops 18874368 | bytes 12582912 | tf_op jit(solution)/shard_map/concatenate | solution.py:19
  46.8 8.6 %copy.21 = bf16[128,24576]{0,1:T(8,128)(2,1)} copy(bf16[128,24576]{1,0:T(8,128)(2,1)} %pad_maximum_fusion) | data formatting | bytes 12582912 | tf_op jit(solution)/shard_map/concatenate | solution.py:19
  55.4 8.7 %copy.22 = bf16[128,192,128]{2,0,1:T(8,128)(2,1)} copy(bf16[128,192,128]{0,2,1:T(8,128)(2,1)} %bitcast.29) | data formatting | bytes 12582912
  64.1 213.0 %while.14 = (s32[]{:T(128)}, f32[128,32,128]{0,2,1:T(8,128)}, pred[32,24]{0,1:T(8,128)(4,1)S(1)}, s32[32,24]{0,1:T(8,128)}, bf16[16,128,128]{2,1,0:T(8,128)(2,1)...) while((s32[]{:T(128)}, f32[128,32,128]{0,2,1:T(8,128)}, ...), condition=%wide.region_1.0_spmd.clone, body=%wide.region_0.0_spmd.clone.sunk | while | flops 136841600 | bytes 10495311 | solution.py:40
  64.8 3.5 %gather_fusion = bf16[32,128,128]{2,1,0:T(8,128)(2,1)S(1)} fusion(bf16[128,192,128]{2,0,1:T(8,128)(2,1)} %get-tuple-element.270, s32[1024]{0:T(1024)S(1)} %pad_clamp_fusion.4), kind=kCustom, calls=%fused_computation.1.clone.clone.1 | custom fusion | bytes 2097280 | tf_op jit(solution)/shard_map/while/body/eval_jaxpr/jit(_take)/gather | solution.py:30
  69.2 2.3 bitcast_add_fusion.2
  72.2 3.5 %gather_fusion = bf16[32,128,128]{2,1,0:T(8,128)(2,1)S(1)} fusion(bf16[128,192,128]{2,0,1:T(8,128)(2,1)} %get-tuple-element.270, s32[1024]{0:T(1024)S(1)} %pad_clamp_fusion.4), kind=kCustom, calls=%fused_computation.1.clone.clone.1 | custom fusion | bytes 2097280 | tf_op jit(solution)/shard_map/while/body/eval_jaxpr/jit(_take)/gather | solution.py:30
  76.5 3.9 %bitcast_add_fusion.2 = f32[128,32,128]{0,2,1:T(8,128)} fusion(f32[128,32,128]{0,2,1:T(8,128)} %get-tuple-element.256, bf16[32,128,128]{2,1,0:T(8,128)(2,1)S(1)} %gather_fusion, bf16[32,128,128]{2,1,0:T(8,128)(2,1)S(1)} %gather_fusion.1, pred[32]{0:T(512)(128)(4,1)S(1)} %get-tuple-element.244, pred[32]{0:T(512)(128)(4,1)S(1)} %get-tuple-element.245, ...), kind=kOutput, calls=%fused_computation.2.clone.1 | convolution fusion | flops 136839168 | bytes 6291553 | tf_op jit(solution)/shard_map/while/body/eval_jaxpr/cnb,nbd->cnd/dot_general | solution.py:35
  81.1 3.5 %gather_fusion = bf16[32,128,128]{2,1,0:T(8,128)(2,1)S(1)} fusion(bf16[128,192,128]{2,0,1:T(8,128)(2,1)} %get-tuple-element.270, s32[1024]{0:T(1024)S(1)} %pad_clamp_fusion.4), kind=kCustom, calls=%fused_computation.1.clone.clone.1 | custom fusion | bytes 2097280 | tf_op jit(solution)/shard_map/while/body/eval_jaxpr/jit(_take)/gather | solution.py:30
  85.5 3.9 %bitcast_add_fusion.2 = f32[128,32,128]{0,2,1:T(8,128)} fusion(f32[128,32,128]{0,2,1:T(8,128)} %get-tuple-element.256, bf16[32,128,128]{2,1,0:T(8,128)(2,1)S(1)} %gather_fusion, bf16[32,128,128]{2,1,0:T(8,128)(2,1)S(1)} %gather_fusion.1, pred[32]{0:T(512)(128)(4,1)S(1)} %get-tuple-element.244, pred[32]{0:T(512)(128)(4,1)S(1)} %get-tuple-element.245, ...), kind=kOutput, calls=%fused_computation.2.clone.1 | convolution fusion | flops 136839168 | bytes 6291553 | tf_op jit(solution)/shard_map/while/body/eval_jaxpr/cnb,nbd->cnd/dot_general | solution.py:35
  90.1 3.5 %gather_fusion = bf16[32,128,128]{2,1,0:T(8,128)(2,1)S(1)} fusion(bf16[128,192,128]{2,0,1:T(8,128)(2,1)} %get-tuple-element.270, s32[1024]{0:T(1024)S(1)} %pad_clamp_fusion.4), kind=kCustom, calls=%fused_computation.1.clone.clone.1 | custom fusion | bytes 2097280 | tf_op jit(solution)/shard_map/while/body/eval_jaxpr/jit(_take)/gather | solution.py:30
  94.4 3.9 %bitcast_add_fusion.2 = f32[128,32,128]{0,2,1:T(8,128)} fusion(f32[128,32,128]{0,2,1:T(8,128)} %get-tuple-element.256, bf16[32,128,128]{2,1,0:T(8,128)(2,1)S(1)} %gather_fusion, bf16[32,128,128]{2,1,0:T(8,128)(2,1)S(1)} %gather_fusion.1, pred[32]{0:T(512)(128)(4,1)S(1)} %get-tuple-element.244, pred[32]{0:T(512)(128)(4,1)S(1)} %get-tuple-element.245, ...), kind=kOutput, calls=%fused_computation.2.clone.1 | convolution fusion | flops 136839168 | bytes 6291553 | tf_op jit(solution)/shard_map/while/body/eval_jaxpr/cnb,nbd->cnd/dot_general | solution.py:35
  99.0 3.5 %gather_fusion = bf16[32,128,128]{2,1,0:T(8,128)(2,1)S(1)} fusion(bf16[128,192,128]{2,0,1:T(8,128)(2,1)} %get-tuple-element.270, s32[1024]{0:T(1024)S(1)} %pad_clamp_fusion.4), kind=kCustom, calls=%fused_computation.1.clone.clone.1 | custom fusion | bytes 2097280 | tf_op jit(solution)/shard_map/while/body/eval_jaxpr/jit(_take)/gather | solution.py:30
  103.4 3.9 %bitcast_add_fusion.2 = f32[128,32,128]{0,2,1:T(8,128)} fusion(f32[128,32,128]{0,2,1:T(8,128)} %get-tuple-element.256, bf16[32,128,128]{2,1,0:T(8,128)(2,1)S(1)} %gather_fusion, bf16[32,128,128]{2,1,0:T(8,128)(2,1)S(1)} %gather_fusion.1, pred[32]{0:T(512)(128)(4,1)S(1)} %get-tuple-element.244, pred[32]{0:T(512)(128)(4,1)S(1)} %get-tuple-element.245, ...), kind=kOutput, calls=%fused_computation.2.clone.1 | convolution fusion | flops 136839168 | bytes 6291553 | tf_op jit(solution)/shard_map/while/body/eval_jaxpr/cnb,nbd->cnd/dot_general | solution.py:35
  108.0 3.5 %gather_fusion = bf16[32,128,128]{2,1,0:T(8,128)(2,1)S(1)} fusion(bf16[128,192,128]{2,0,1:T(8,128)(2,1)} %get-tuple-element.270, s32[1024]{0:T(1024)S(1)} %pad_clamp_fusion.4), kind=kCustom, calls=%fused_computation.1.clone.clone.1 | custom fusion | bytes 2097280 | tf_op jit(solution)/shard_map/while/body/eval_jaxpr/jit(_take)/gather | solution.py:30
  112.3 3.9 %bitcast_add_fusion.2 = f32[128,32,128]{0,2,1:T(8,128)} fusion(f32[128,32,128]{0,2,1:T(8,128)} %get-tuple-element.256, bf16[32,128,128]{2,1,0:T(8,128)(2,1)S(1)} %gather_fusion, bf16[32,128,128]{2,1,0:T(8,128)(2,1)S(1)} %gather_fusion.1, pred[32]{0:T(512)(128)(4,1)S(1)} %get-tuple-element.244, pred[32]{0:T(512)(128)(4,1)S(1)} %get-tuple-element.245, ...), kind=kOutput, calls=%fused_computation.2.clone.1 | convolution fusion | flops 136839168 | bytes 6291553 | tf_op jit(solution)/shard_map/while/body/eval_jaxpr/cnb,nbd->cnd/dot_general | solution.py:35
  116.9 3.5 %gather_fusion = bf16[32,128,128]{2,1,0:T(8,128)(2,1)S(1)} fusion(bf16[128,192,128]{2,0,1:T(8,128)(2,1)} %get-tuple-element.270, s32[1024]{0:T(1024)S(1)} %pad_clamp_fusion.4), kind=kCustom, calls=%fused_computation.1.clone.clone.1 | custom fusion | bytes 2097280 | tf_op jit(solution)/shard_map/while/body/eval_jaxpr/jit(_take)/gather | solution.py:30
  121.2 3.9 %bitcast_add_fusion.2 = f32[128,32,128]{0,2,1:T(8,128)} fusion(f32[128,32,128]{0,2,1:T(8,128)} %get-tuple-element.256, bf16[32,128,128]{2,1,0:T(8,128)(2,1)S(1)} %gather_fusion, bf16[32,128,128]{2,1,0:T(8,128)(2,1)S(1)} %gather_fusion.1, pred[32]{0:T(512)(128)(4,1)S(1)} %get-tuple-element.244, pred[32]{0:T(512)(128)(4,1)S(1)} %get-tuple-element.245, ...), kind=kOutput, calls=%fused_computation.2.clone.1 | convolution fusion | flops 136839168 | bytes 6291553 | tf_op jit(solution)/shard_map/while/body/eval_jaxpr/cnb,nbd->cnd/dot_general | solution.py:35
  125.8 3.5 %gather_fusion = bf16[32,128,128]{2,1,0:T(8,128)(2,1)S(1)} fusion(bf16[128,192,128]{2,0,1:T(8,128)(2,1)} %get-tuple-element.270, s32[1024]{0:T(1024)S(1)} %pad_clamp_fusion.4), kind=kCustom, calls=%fused_computation.1.clone.clone.1 | custom fusion | bytes 2097280 | tf_op jit(solution)/shard_map/while/body/eval_jaxpr/jit(_take)/gather | solution.py:30
  130.2 3.9 %bitcast_add_fusion.2 = f32[128,32,128]{0,2,1:T(8,128)} fusion(f32[128,32,128]{0,2,1:T(8,128)} %get-tuple-element.256, bf16[32,128,128]{2,1,0:T(8,128)(2,1)S(1)} %gather_fusion, bf16[32,128,128]{2,1,0:T(8,128)(2,1)S(1)} %gather_fusion.1, pred[32]{0:T(512)(128)(4,1)S(1)} %get-tuple-element.244, pred[32]{0:T(512)(128)(4,1)S(1)} %get-tuple-element.245, ...), kind=kOutput, calls=%fused_computation.2.clone.1 | convolution fusion | flops 136839168 | bytes 6291553 | tf_op jit(solution)/shard_map/while/body/eval_jaxpr/cnb,nbd->cnd/dot_general | solution.py:35
  134.8 3.5 %gather_fusion = bf16[32,128,128]{2,1,0:T(8,128)(2,1)S(1)} fusion(bf16[128,192,128]{2,0,1:T(8,128)(2,1)} %get-tuple-element.270, s32[1024]{0:T(1024)S(1)} %pad_clamp_fusion.4), kind=kCustom, calls=%fused_computation.1.clone.clone.1 | custom fusion | bytes 2097280 | tf_op jit(solution)/shard_map/while/body/eval_jaxpr/jit(_take)/gather | solution.py:30
  139.1 3.9 %bitcast_add_fusion.2 = f32[128,32,128]{0,2,1:T(8,128)} fusion(f32[128,32,128]{0,2,1:T(8,128)} %get-tuple-element.256, bf16[32,128,128]{2,1,0:T(8,128)(2,1)S(1)} %gather_fusion, bf16[32,128,128]{2,1,0:T(8,128)(2,1)S(1)} %gather_fusion.1, pred[32]{0:T(512)(128)(4,1)S(1)} %get-tuple-element.244, pred[32]{0:T(512)(128)(4,1)S(1)} %get-tuple-element.245, ...), kind=kOutput, calls=%fused_computation.2.clone.1 | convolution fusion | flops 136839168 | bytes 6291553 | tf_op jit(solution)/shard_map/while/body/eval_jaxpr/cnb,nbd->cnd/dot_general | solution.py:35
  143.7 3.5 %gather_fusion = bf16[32,128,128]{2,1,0:T(8,128)(2,1)S(1)} fusion(bf16[128,192,128]{2,0,1:T(8,128)(2,1)} %get-tuple-element.270, s32[1024]{0:T(1024)S(1)} %pad_clamp_fusion.4), kind=kCustom, calls=%fused_computation.1.clone.clone.1 | custom fusion | bytes 2097280 | tf_op jit(solution)/shard_map/while/body/eval_jaxpr/jit(_take)/gather | solution.py:30
  148.1 3.9 %bitcast_add_fusion.2 = f32[128,32,128]{0,2,1:T(8,128)} fusion(f32[128,32,128]{0,2,1:T(8,128)} %get-tuple-element.256, bf16[32,128,128]{2,1,0:T(8,128)(2,1)S(1)} %gather_fusion, bf16[32,128,128]{2,1,0:T(8,128)(2,1)S(1)} %gather_fusion.1, pred[32]{0:T(512)(128)(4,1)S(1)} %get-tuple-element.244, pred[32]{0:T(512)(128)(4,1)S(1)} %get-tuple-element.245, ...), kind=kOutput, calls=%fused_computation.2.clone.1 | convolution fusion | flops 136839168 | bytes 6291553 | tf_op jit(solution)/shard_map/while/body/eval_jaxpr/cnb,nbd->cnd/dot_general | solution.py:35
  152.7 3.5 %gather_fusion = bf16[32,128,128]{2,1,0:T(8,128)(2,1)S(1)} fusion(bf16[128,192,128]{2,0,1:T(8,128)(2,1)} %get-tuple-element.270, s32[1024]{0:T(1024)S(1)} %pad_clamp_fusion.4), kind=kCustom, calls=%fused_computation.1.clone.clone.1 | custom fusion | bytes 2097280 | tf_op jit(solution)/shard_map/while/body/eval_jaxpr/jit(_take)/gather | solution.py:30
  157.0 3.9 %bitcast_add_fusion.2 = f32[128,32,128]{0,2,1:T(8,128)} fusion(f32[128,32,128]{0,2,1:T(8,128)} %get-tuple-element.256, bf16[32,128,128]{2,1,0:T(8,128)(2,1)S(1)} %gather_fusion, bf16[32,128,128]{2,1,0:T(8,128)(2,1)S(1)} %gather_fusion.1, pred[32]{0:T(512)(128)(4,1)S(1)} %get-tuple-element.244, pred[32]{0:T(512)(128)(4,1)S(1)} %get-tuple-element.245, ...), kind=kOutput, calls=%fused_computation.2.clone.1 | convolution fusion | flops 136839168 | bytes 6291553 | tf_op jit(solution)/shard_map/while/body/eval_jaxpr/cnb,nbd->cnd/dot_general | solution.py:35
  161.6 3.5 %gather_fusion = bf16[32,128,128]{2,1,0:T(8,128)(2,1)S(1)} fusion(bf16[128,192,128]{2,0,1:T(8,128)(2,1)} %get-tuple-element.270, s32[1024]{0:T(1024)S(1)} %pad_clamp_fusion.4), kind=kCustom, calls=%fused_computation.1.clone.clone.1 | custom fusion | bytes 2097280 | tf_op jit(solution)/shard_map/while/body/eval_jaxpr/jit(_take)/gather | solution.py:30
  166.0 3.9 %bitcast_add_fusion.2 = f32[128,32,128]{0,2,1:T(8,128)} fusion(f32[128,32,128]{0,2,1:T(8,128)} %get-tuple-element.256, bf16[32,128,128]{2,1,0:T(8,128)(2,1)S(1)} %gather_fusion, bf16[32,128,128]{2,1,0:T(8,128)(2,1)S(1)} %gather_fusion.1, pred[32]{0:T(512)(128)(4,1)S(1)} %get-tuple-element.244, pred[32]{0:T(512)(128)(4,1)S(1)} %get-tuple-element.245, ...), kind=kOutput, calls=%fused_computation.2.clone.1 | convolution fusion | flops 136839168 | bytes 6291553 | tf_op jit(solution)/shard_map/while/body/eval_jaxpr/cnb,nbd->cnd/dot_general | solution.py:35
  170.6 3.5 %gather_fusion = bf16[32,128,128]{2,1,0:T(8,128)(2,1)S(1)} fusion(bf16[128,192,128]{2,0,1:T(8,128)(2,1)} %get-tuple-element.270, s32[1024]{0:T(1024)S(1)} %pad_clamp_fusion.4), kind=kCustom, calls=%fused_computation.1.clone.clone.1 | custom fusion | bytes 2097280 | tf_op jit(solution)/shard_map/while/body/eval_jaxpr/jit(_take)/gather | solution.py:30
  174.9 3.9 %bitcast_add_fusion.2 = f32[128,32,128]{0,2,1:T(8,128)} fusion(f32[128,32,128]{0,2,1:T(8,128)} %get-tuple-element.256, bf16[32,128,128]{2,1,0:T(8,128)(2,1)S(1)} %gather_fusion, bf16[32,128,128]{2,1,0:T(8,128)(2,1)S(1)} %gather_fusion.1, pred[32]{0:T(512)(128)(4,1)S(1)} %get-tuple-element.244, pred[32]{0:T(512)(128)(4,1)S(1)} %get-tuple-element.245, ...), kind=kOutput, calls=%fused_computation.2.clone.1 | convolution fusion | flops 136839168 | bytes 6291553 | tf_op jit(solution)/shard_map/while/body/eval_jaxpr/cnb,nbd->cnd/dot_general | solution.py:35
  179.5 3.5 %gather_fusion = bf16[32,128,128]{2,1,0:T(8,128)(2,1)S(1)} fusion(bf16[128,192,128]{2,0,1:T(8,128)(2,1)} %get-tuple-element.270, s32[1024]{0:T(1024)S(1)} %pad_clamp_fusion.4), kind=kCustom, calls=%fused_computation.1.clone.clone.1 | custom fusion | bytes 2097280 | tf_op jit(solution)/shard_map/while/body/eval_jaxpr/jit(_take)/gather | solution.py:30
  183.8 3.9 %bitcast_add_fusion.2 = f32[128,32,128]{0,2,1:T(8,128)} fusion(f32[128,32,128]{0,2,1:T(8,128)} %get-tuple-element.256, bf16[32,128,128]{2,1,0:T(8,128)(2,1)S(1)} %gather_fusion, bf16[32,128,128]{2,1,0:T(8,128)(2,1)S(1)} %gather_fusion.1, pred[32]{0:T(512)(128)(4,1)S(1)} %get-tuple-element.244, pred[32]{0:T(512)(128)(4,1)S(1)} %get-tuple-element.245, ...), kind=kOutput, calls=%fused_computation.2.clone.1 | convolution fusion | flops 136839168 | bytes 6291553 | tf_op jit(solution)/shard_map/while/body/eval_jaxpr/cnb,nbd->cnd/dot_general | solution.py:35
  188.4 3.5 %gather_fusion = bf16[32,128,128]{2,1,0:T(8,128)(2,1)S(1)} fusion(bf16[128,192,128]{2,0,1:T(8,128)(2,1)} %get-tuple-element.270, s32[1024]{0:T(1024)S(1)} %pad_clamp_fusion.4), kind=kCustom, calls=%fused_computation.1.clone.clone.1 | custom fusion | bytes 2097280 | tf_op jit(solution)/shard_map/while/body/eval_jaxpr/jit(_take)/gather | solution.py:30
  192.8 3.9 %bitcast_add_fusion.2 = f32[128,32,128]{0,2,1:T(8,128)} fusion(f32[128,32,128]{0,2,1:T(8,128)} %get-tuple-element.256, bf16[32,128,128]{2,1,0:T(8,128)(2,1)S(1)} %gather_fusion, bf16[32,128,128]{2,1,0:T(8,128)(2,1)S(1)} %gather_fusion.1, pred[32]{0:T(512)(128)(4,1)S(1)} %get-tuple-element.244, pred[32]{0:T(512)(128)(4,1)S(1)} %get-tuple-element.245, ...), kind=kOutput, calls=%fused_computation.2.clone.1 | convolution fusion | flops 136839168 | bytes 6291553 | tf_op jit(solution)/shard_map/while/body/eval_jaxpr/cnb,nbd->cnd/dot_general | solution.py:35
  197.4 3.5 %gather_fusion = bf16[32,128,128]{2,1,0:T(8,128)(2,1)S(1)} fusion(bf16[128,192,128]{2,0,1:T(8,128)(2,1)} %get-tuple-element.270, s32[1024]{0:T(1024)S(1)} %pad_clamp_fusion.4), kind=kCustom, calls=%fused_computation.1.clone.clone.1 | custom fusion | bytes 2097280 | tf_op jit(solution)/shard_map/while/body/eval_jaxpr/jit(_take)/gather | solution.py:30
  201.7 3.9 %bitcast_add_fusion.2 = f32[128,32,128]{0,2,1:T(8,128)} fusion(f32[128,32,128]{0,2,1:T(8,128)} %get-tuple-element.256, bf16[32,128,128]{2,1,0:T(8,128)(2,1)S(1)} %gather_fusion, bf16[32,128,128]{2,1,0:T(8,128)(2,1)S(1)} %gather_fusion.1, pred[32]{0:T(512)(128)(4,1)S(1)} %get-tuple-element.244, pred[32]{0:T(512)(128)(4,1)S(1)} %get-tuple-element.245, ...), kind=kOutput, calls=%fused_computation.2.clone.1 | convolution fusion | flops 136839168 | bytes 6291553 | tf_op jit(solution)/shard_map/while/body/eval_jaxpr/cnb,nbd->cnd/dot_general | solution.py:35
  206.3 3.5 %gather_fusion = bf16[32,128,128]{2,1,0:T(8,128)(2,1)S(1)} fusion(bf16[128,192,128]{2,0,1:T(8,128)(2,1)} %get-tuple-element.270, s32[1024]{0:T(1024)S(1)} %pad_clamp_fusion.4), kind=kCustom, calls=%fused_computation.1.clone.clone.1 | custom fusion | bytes 2097280 | tf_op jit(solution)/shard_map/while/body/eval_jaxpr/jit(_take)/gather | solution.py:30
  210.7 3.9 %bitcast_add_fusion.2 = f32[128,32,128]{0,2,1:T(8,128)} fusion(f32[128,32,128]{0,2,1:T(8,128)} %get-tuple-element.256, bf16[32,128,128]{2,1,0:T(8,128)(2,1)S(1)} %gather_fusion, bf16[32,128,128]{2,1,0:T(8,128)(2,1)S(1)} %gather_fusion.1, pred[32]{0:T(512)(128)(4,1)S(1)} %get-tuple-element.244, pred[32]{0:T(512)(128)(4,1)S(1)} %get-tuple-element.245, ...), kind=kOutput, calls=%fused_computation.2.clone.1 | convolution fusion | flops 136839168 | bytes 6291553 | tf_op jit(solution)/shard_map/while/body/eval_jaxpr/cnb,nbd->cnd/dot_general | solution.py:35
  215.3 3.5 %gather_fusion = bf16[32,128,128]{2,1,0:T(8,128)(2,1)S(1)} fusion(bf16[128,192,128]{2,0,1:T(8,128)(2,1)} %get-tuple-element.270, s32[1024]{0:T(1024)S(1)} %pad_clamp_fusion.4), kind=kCustom, calls=%fused_computation.1.clone.clone.1 | custom fusion | bytes 2097280 | tf_op jit(solution)/shard_map/while/body/eval_jaxpr/jit(_take)/gather | solution.py:30
  219.6 3.9 %bitcast_add_fusion.2 = f32[128,32,128]{0,2,1:T(8,128)} fusion(f32[128,32,128]{0,2,1:T(8,128)} %get-tuple-element.256, bf16[32,128,128]{2,1,0:T(8,128)(2,1)S(1)} %gather_fusion, bf16[32,128,128]{2,1,0:T(8,128)(2,1)S(1)} %gather_fusion.1, pred[32]{0:T(512)(128)(4,1)S(1)} %get-tuple-element.244, pred[32]{0:T(512)(128)(4,1)S(1)} %get-tuple-element.245, ...), kind=kOutput, calls=%fused_computation.2.clone.1 | convolution fusion | flops 136839168 | bytes 6291553 | tf_op jit(solution)/shard_map/while/body/eval_jaxpr/cnb,nbd->cnd/dot_general | solution.py:35
  224.2 3.5 %gather_fusion = bf16[32,128,128]{2,1,0:T(8,128)(2,1)S(1)} fusion(bf16[128,192,128]{2,0,1:T(8,128)(2,1)} %get-tuple-element.270, s32[1024]{0:T(1024)S(1)} %pad_clamp_fusion.4), kind=kCustom, calls=%fused_computation.1.clone.clone.1 | custom fusion | bytes 2097280 | tf_op jit(solution)/shard_map/while/body/eval_jaxpr/jit(_take)/gather | solution.py:30
  228.6 3.9 %bitcast_add_fusion.2 = f32[128,32,128]{0,2,1:T(8,128)} fusion(f32[128,32,128]{0,2,1:T(8,128)} %get-tuple-element.256, bf16[32,128,128]{2,1,0:T(8,128)(2,1)S(1)} %gather_fusion, bf16[32,128,128]{2,1,0:T(8,128)(2,1)S(1)} %gather_fusion.1, pred[32]{0:T(512)(128)(4,1)S(1)} %get-tuple-element.244, pred[32]{0:T(512)(128)(4,1)S(1)} %get-tuple-element.245, ...), kind=kOutput, calls=%fused_computation.2.clone.1 | convolution fusion | flops 136839168 | bytes 6291553 | tf_op jit(solution)/shard_map/while/body/eval_jaxpr/cnb,nbd->cnd/dot_general | solution.py:35
  233.2 3.5 %gather_fusion = bf16[32,128,128]{2,1,0:T(8,128)(2,1)S(1)} fusion(bf16[128,192,128]{2,0,1:T(8,128)(2,1)} %get-tuple-element.270, s32[1024]{0:T(1024)S(1)} %pad_clamp_fusion.4), kind=kCustom, calls=%fused_computation.1.clone.clone.1 | custom fusion | bytes 2097280 | tf_op jit(solution)/shard_map/while/body/eval_jaxpr/jit(_take)/gather | solution.py:30
  237.5 3.9 %bitcast_add_fusion.2 = f32[128,32,128]{0,2,1:T(8,128)} fusion(f32[128,32,128]{0,2,1:T(8,128)} %get-tuple-element.256, bf16[32,128,128]{2,1,0:T(8,128)(2,1)S(1)} %gather_fusion, bf16[32,128,128]{2,1,0:T(8,128)(2,1)S(1)} %gather_fusion.1, pred[32]{0:T(512)(128)(4,1)S(1)} %get-tuple-element.244, pred[32]{0:T(512)(128)(4,1)S(1)} %get-tuple-element.245, ...), kind=kOutput, calls=%fused_computation.2.clone.1 | convolution fusion | flops 136839168 | bytes 6291553 | tf_op jit(solution)/shard_map/while/body/eval_jaxpr/cnb,nbd->cnd/dot_general | solution.py:35
  242.1 3.5 %gather_fusion = bf16[32,128,128]{2,1,0:T(8,128)(2,1)S(1)} fusion(bf16[128,192,128]{2,0,1:T(8,128)(2,1)} %get-tuple-element.270, s32[1024]{0:T(1024)S(1)} %pad_clamp_fusion.4), kind=kCustom, calls=%fused_computation.1.clone.clone.1 | custom fusion | bytes 2097280 | tf_op jit(solution)/shard_map/while/body/eval_jaxpr/jit(_take)/gather | solution.py:30
  246.4 3.9 %bitcast_add_fusion.2 = f32[128,32,128]{0,2,1:T(8,128)} fusion(f32[128,32,128]{0,2,1:T(8,128)} %get-tuple-element.256, bf16[32,128,128]{2,1,0:T(8,128)(2,1)S(1)} %gather_fusion, bf16[32,128,128]{2,1,0:T(8,128)(2,1)S(1)} %gather_fusion.1, pred[32]{0:T(512)(128)(4,1)S(1)} %get-tuple-element.244, pred[32]{0:T(512)(128)(4,1)S(1)} %get-tuple-element.245, ...), kind=kOutput, calls=%fused_computation.2.clone.1 | convolution fusion | flops 136839168 | bytes 6291553 | tf_op jit(solution)/shard_map/while/body/eval_jaxpr/cnb,nbd->cnd/dot_general | solution.py:35
  251.0 3.5 %gather_fusion = bf16[32,128,128]{2,1,0:T(8,128)(2,1)S(1)} fusion(bf16[128,192,128]{2,0,1:T(8,128)(2,1)} %get-tuple-element.270, s32[1024]{0:T(1024)S(1)} %pad_clamp_fusion.4), kind=kCustom, calls=%fused_computation.1.clone.clone.1 | custom fusion | bytes 2097280 | tf_op jit(solution)/shard_map/while/body/eval_jaxpr/jit(_take)/gather | solution.py:30
  255.4 3.9 %bitcast_add_fusion.2 = f32[128,32,128]{0,2,1:T(8,128)} fusion(f32[128,32,128]{0,2,1:T(8,128)} %get-tuple-element.256, bf16[32,128,128]{2,1,0:T(8,128)(2,1)S(1)} %gather_fusion, bf16[32,128,128]{2,1,0:T(8,128)(2,1)S(1)} %gather_fusion.1, pred[32]{0:T(512)(128)(4,1)S(1)} %get-tuple-element.244, pred[32]{0:T(512)(128)(4,1)S(1)} %get-tuple-element.245, ...), kind=kOutput, calls=%fused_computation.2.clone.1 | convolution fusion | flops 136839168 | bytes 6291553 | tf_op jit(solution)/shard_map/while/body/eval_jaxpr/cnb,nbd->cnd/dot_general | solution.py:35
  260.0 3.5 %gather_fusion = bf16[32,128,128]{2,1,0:T(8,128)(2,1)S(1)} fusion(bf16[128,192,128]{2,0,1:T(8,128)(2,1)} %get-tuple-element.270, s32[1024]{0:T(1024)S(1)} %pad_clamp_fusion.4), kind=kCustom, calls=%fused_computation.1.clone.clone.1 | custom fusion | bytes 2097280 | tf_op jit(solution)/shard_map/while/body/eval_jaxpr/jit(_take)/gather | solution.py:30
  264.3 3.9 %bitcast_add_fusion.2 = f32[128,32,128]{0,2,1:T(8,128)} fusion(f32[128,32,128]{0,2,1:T(8,128)} %get-tuple-element.256, bf16[32,128,128]{2,1,0:T(8,128)(2,1)S(1)} %gather_fusion, bf16[32,128,128]{2,1,0:T(8,128)(2,1)S(1)} %gather_fusion.1, pred[32]{0:T(512)(128)(4,1)S(1)} %get-tuple-element.244, pred[32]{0:T(512)(128)(4,1)S(1)} %get-tuple-element.245, ...), kind=kOutput, calls=%fused_computation.2.clone.1 | convolution fusion | flops 136839168 | bytes 6291553 | tf_op jit(solution)/shard_map/while/body/eval_jaxpr/cnb,nbd->cnd/dot_general | solution.py:35
  268.9 3.5 %gather_fusion = bf16[32,128,128]{2,1,0:T(8,128)(2,1)S(1)} fusion(bf16[128,192,128]{2,0,1:T(8,128)(2,1)} %get-tuple-element.270, s32[1024]{0:T(1024)S(1)} %pad_clamp_fusion.4), kind=kCustom, calls=%fused_computation.1.clone.clone.1 | custom fusion | bytes 2097280 | tf_op jit(solution)/shard_map/while/body/eval_jaxpr/jit(_take)/gather | solution.py:30
  273.3 3.9 %bitcast_add_fusion.2 = f32[128,32,128]{0,2,1:T(8,128)} fusion(f32[128,32,128]{0,2,1:T(8,128)} %get-tuple-element.256, bf16[32,128,128]{2,1,0:T(8,128)(2,1)S(1)} %gather_fusion, bf16[32,128,128]{2,1,0:T(8,128)(2,1)S(1)} %gather_fusion.1, pred[32]{0:T(512)(128)(4,1)S(1)} %get-tuple-element.244, pred[32]{0:T(512)(128)(4,1)S(1)} %get-tuple-element.245, ...), kind=kOutput, calls=%fused_computation.2.clone.1 | convolution fusion | flops 136839168 | bytes 6291553 | tf_op jit(solution)/shard_map/while/body/eval_jaxpr/cnb,nbd->cnd/dot_general | solution.py:35
  277.2 2.1 reduce_sum.40
  279.3 2.4 copy.23
  281.7 10.5 %all-reduce = (f32[128]{0:T(128)S(1)}, f32[128]{0:T(128)S(1)}, f32[]{:T(128)}) all-reduce(f32[128]{0:T(128)S(1)} %reduce_sum.39, f32[128]{0:T(128)S(1)} %reduce_sum.40, f32[]{:T(128)} %reduce_sum.41), channel_id=1, replica_groups=mesh['grp'=2,'band'=4,'mem'=2,'fld'=2] {'band'}, use_global_device_ids=true, to_apply=%region_3.0 | all-reduce | flops 257 | bytes 2056 | tf_op jit(solution)/shard_map/psum | solution.py:44
  293.0 1.5 reshape.50
  294.6 4.9 %psum.31 = f32[4,8]{1,0:T(4,128)S(1)} all-reduce(f32[4,8]{1,0:T(4,128)S(1)} %reduce_sum.42), channel_id=1, replica_groups=mesh['grp'=2,'band'=4,'mem'=2,'fld'=2] {'mem'}, use_global_device_ids=true, to_apply=%region_9.10 | all-reduce | flops 32 | bytes 256 | tf_op jit(solution)/shard_map/psum | solution.py:75
  300.1 3.2 %divide_add_fusion = f32[4,4,8,4096]{3,2,1,0:T(8,128)} fusion(f32[4,4,8,4096]{3,2,1,0:T(8,128)} %reshape.50, f32[4,4,8]{2,1,0:T(4,128)S(1)} %add.85, f32[4096]{0:T(1024)S(1)} %copy-done.2), kind=kLoop, calls=%fused_computation.26 | loop fusion | flops 1048576 | bytes 4211200 | tf_op jit(solution)/shard_map/add | solution.py:73
  (140 shorter events, 39.9 us)
Async XLA Ops:
  5.3 2.0 copy-start.1
  5.3 9.6 %copy-start.2 = (f32[4096]{0:T(1024)S(1)}, f32[4096]{0:T(1024)}, u32[]{:S(2)}) copy-start(f32[4096]{0:T(1024)} %param.13) | copy-start | bytes 49156
  5.3 10.2 %copy-start.4 = (s32[32]{0:T(128)S(1)}, s32[32]{0:T(128)}, u32[]{:S(2)}) copy-start(s32[32]{0:T(128)} %param.17) | copy-start | bytes 388
  8.5 27.7 %collective-permute-start = (bf16[128,4096]{1,0:T(8,128)(2,1)}, bf16[128,4096]{1,0:T(8,128)(2,1)S(1)}, u32[]{:S(2)}, u32[]{:S(2)}) collective-permute-start(bf16[128,4096]{1,0:T(8,128)(2,1)} %get-tuple-element.191), channel_id=1, source_target_pairs={{0,4},{4,8},{8,12},{1,5},{5,9},{9,13},{2,6},{6,10},{10,14},{3,7},{... | collective-permute-start | bytes 3145736 | tf_op jit(solution)/shard_map/ppermute | solution.py:17
  13.5 26.5 %collective-permute-start.1 = (bf16[128,4096]{1,0:T(8,128)(2,1)S(1)}, bf16[128,4096]{1,0:T(8,128)(2,1)S(1)}, u32[]{:S(2)}, u32[]{:S(2)}) collective-permute-start(bf16[128,4096]{1,0:T(8,128)(2,1)S(1)} %get-tuple-element.192), channel_id=1, source_target_pairs={{4,0},{8,4},{12,8},{5,1},{9,5},{13,9},{6,2},{10,6},{14,10},{7,3},{... | collective-permute-start | bytes 3145736 | tf_op jit(solution)/shard_map/ppermute | solution.py:18
  55.4 8.7 %copy-start = (bf16[16,128,128]{2,1,0:T(8,128)(2,1)S(1)}, bf16[16,128,128]{2,1,0:T(8,128)(2,1)}, u32[]{:S(2)}) copy-start(bf16[16,128,128]{2,1,0:T(8,128)(2,1)} %param.14) | copy-start | bytes 1572868
  294.6 8.7 %copy-start.3 = (f32[4,4,8]{2,1,0:T(4,128)}, f32[4,4,8]{2,1,0:T(4,128)S(1)}, u32[]{:S(2)}) copy-start(f32[4,4,8]{2,1,0:T(4,128)S(1)} %reshape.51) | copy-start | bytes 1540
where the time goes:
time: 306 us; the launch traced here: 303 us
  local copies, waits for them, and re-layouts  128 us (42%)
  matrix products  91.6 us (30%)
  other arithmetic  35.9 us (12%)
  waiting for transfers between devices  24.5 us (8%)
  blocking collectives  15.5 us (5%)
  starting transfers between devices  6.3 us (2%)
    dot_general x24, matrix products, one_slot(): jnp.einsum('cnb,nbd->cnd', chosen, weights, preferred_element_type=jnp.fl...  91.6 us
    gather x24, local copies, waits for them, and re-layouts, one_slot(): chosen = jnp.take(source, picked[:, position], axis=1)  84.8 us
    ppermute x1, waiting for transfers between devices, extended_2(): before = lax.ppermute(last, axis, up)  20.6 us
    gather x24, local copies, waits for them, and re-layouts, one_slot(): weights = jnp.take(weight_tiles, tile_ids[:, position], axis=0)  18 us
    reduce_and x24, other arithmetic, one_slot(): chosen = jnp.take(source, picked[:, position], axis=1)  17.1 us
    unnamed x11, local copies, waits for them, and re-layouts  10.8 us
    psum x1, blocking collectives, band_totals(): return lax.psum((own_total, target_part, area_part), 'band')  10.5 us
    concatenate x1, local copies, waits for them, and re-layouts, extended_2(): array = jnp.concatenate([before, array, after], axis=dim)  8.62 us
  transfers between devices with their start and end apart: 2, of which 2 were waited for; matrix products, arithmetic and copies ran while one was open for 0% of the time, Pallas kernels for 0%

commit v1 on v0

v1 whole, which is shorter than its diff:
```python
import functools

import jax
import jax.numpy as jnp
from jax import lax
from jax.experimental import pallas as pl
from jax.experimental.pallas import tpu as pltpu
from jax.sharding import PartitionSpec as P


MEMBERS = 8
HALO_BLK = 32
CHUNK = 4
UNROLL = 4
PIECES = 8
PLACE_BITS = 16

VMEM = pl.BlockSpec(memory_space=pltpu.VMEM)
SMEM = pl.BlockSpec(memory_space=pltpu.SMEM)
ANY = pl.BlockSpec(memory_space=pl.ANY)


def params(mib):
    return pltpu.CompilerParams(vmem_limit_bytes=mib * 1024 * 1024)


def row_of(acc):
    return jnp.sum(acc.T, axis=0, keepdims=True)


def list_items(tile_of, block_of, live, columns, bounds, shift, blank, at, out):
    slots = tile_of.shape[0]
    last = out.shape[1] - 1

    def one_target(n, items):
        column = columns + n

        def one_slot(k, place):
            block = block_of[k, column] - HALO_BLK
            out[0, place] = (tile_of[k, column] << PLACE_BITS) + block + shift
            inside = jnp.logical_and(block >= bounds[0], block < bounds[1])
            return place + jnp.where(inside, 1, 0)

        place = lax.fori_loop(0, live[column], one_slot, items * CHUNK)
        for q in range(CHUNK):
            out[0, place + q] = blank
        for q in range(-(-slots // CHUNK)):
            out[0, at + items + q] = n
        return lax.div(place + CHUNK - 1, CHUNK)

    def listed(count):
        items = lax.fori_loop(0, count, one_target, 0)
        for q in range(UNROLL * CHUNK):
            out[0, items * CHUNK + q] = blank
        for q in range(UNROLL):
            out[0, at + items + q] = 0
        out[0, last] = items

    return listed


def list_sizes(targets, slots):
    items = targets * -(-slots // CHUNK) + UNROLL
    at = items * CHUNK
    return at, -(-(at + items + 8) // 128) * 128


def edge_body(own_blocks, blank, edge, tile_of, block_of, live, low, high):
    slots, tgt_count = tile_of.shape
    at, _ = list_sizes(edge, slots)
    list_items(
        tile_of, block_of, live, 0, (-HALO_BLK, 0), own_blocks, blank, at, low
    )(edge)
    list_items(
        tile_of, block_of, live, tgt_count - edge, (own_blocks, own_blocks + HALO_BLK),
        -own_blocks, blank, at, high,
    )(edge)


def weigh_body(
    fields_hbm, mask_ref, area_ref, target_ref, tiles_hbm, tile_of, block_of, live,
    weighted, tiles, totals, items, staged, sems,
):
    columns, cells = weighted.shape
    tile_count, tile, lanes = tiles_hbm.shape
    own_blocks = cells // tile
    slots, tgt_count = tile_of.shape
    piece = cells // PIECES
    step = 4 * tile
    copies = [
        pltpu.make_async_copy(
            fields_hbm.at[:, pl.ds(n * piece, piece)],
            staged.at[:, pl.ds(n * piece, piece)],
            sems.at[n],
        )
        for n in range(PIECES)
    ]
    for copy in copies:
        copy.start()
    tile_copy = pltpu.make_async_copy(tiles_hbm, tiles.at[pl.ds(0, tile_count)], sems.at[PIECES])
    tile_copy.start()
    tiles[tile_count] = jnp.zeros((tile, lanes), tiles.dtype)
    at, _ = list_sizes(tgt_count, slots)
    list_items(
        tile_of, block_of, live, 0, (0, own_blocks), 0, tile_count << PLACE_BITS, at, items
    )(tgt_count)
    acc = jnp.zeros((columns, tile), jnp.float32)
    for n in range(PIECES):
        copies[n].wait()

        def one(k, acc):
            at = pl.ds(pl.multiple_of(n * piece + k * step, step), step)
            factor = area_ref[:, at] * mask_ref[:, at].astype(jnp.float32)
            value = (factor * staged[:, at].astype(jnp.float32)).astype(jnp.bfloat16)
            weighted[:, at] = value
            wide = value.astype(jnp.float32)
            for q in range(4):
                acc = acc + wide[:, q * tile : (q + 1) * tile]
            return acc

        acc = lax.fori_loop(0, piece // step, one, acc)
    own = row_of(acc)
    area = jnp.sum(target_ref[...], axis=1, keepdims=True)
    rows = lax.broadcasted_iota(jnp.int32, (8, columns), 0)
    totals[...] = jnp.where(rows == 0, own, jnp.where(rows == 1, area, 0.0))
    tile_copy.wait()


def run_items(items, at, weighted, tiles, out):
    tile = tiles.shape[1]
    count = items[0, items.shape[1] - 1]
    out[...] = jnp.zeros(out.shape, out.dtype)

    def one(step, nothing):
        base = step * UNROLL
        products = []
        for u in range(UNROLL):
            left, right = [], []
            for q in range(CHUNK):
                code = items[0, (base + u) * CHUNK + q]
                block = code & ((1 << PLACE_BITS) - 1)
                left.append(weighted[:, pl.ds(pl.multiple_of(block * tile, tile), tile)])
                right.append(tiles[code >> PLACE_BITS])
            products.append(
                jnp.dot(
                    jnp.concatenate(left, axis=1),
                    jnp.concatenate(right, axis=0),
                    preferred_element_type=jnp.float32,
                )
            )
        for u in range(UNROLL):
            target = items[0, at + base + u]
            place = pl.ds(pl.multiple_of(target * tile, tile), tile)
            out[:, place] = out[:, place] + products[u]
        return nothing

    lax.fori_loop(0, lax.div(count + UNROLL - 1, UNROLL), one, 0)
    acc = out[:, :tile]
    for n in range(1, out.shape[1] // tile):
        acc = acc + out[:, n * tile : (n + 1) * tile]
    return acc


def reach_body(at, up_items, down_items, weighted, tiles, to_up, to_down, sums, first, second):
    acc = run_items(up_items, at, weighted, tiles, first)
    to_up[...] = first[...].astype(to_up.dtype)
    acc = acc + run_items(down_items, at, weighted, tiles, second)
    to_down[...] = second[...].astype(to_down.dtype)
    sums[...] = jnp.broadcast_to(row_of(acc), sums.shape)


def local_body(at, items, weighted, tiles, reach_sums, raw, sums):
    acc = run_items(items, at, weighted, tiles, raw)
    sums[...] = reach_sums[...] + row_of(acc)


def finish_body(raw, from_down, from_up, target, totals, sums, out_hbm, staged, sems):
    columns, cells = raw.shape
    edge = from_down.shape[1]
    piece = edge // 2
    pieces = cells // piece
    correction = (totals[0:1] - sums[0:1]) / totals[1:2]
    spread = jnp.broadcast_to(correction, (128, columns)).T
    spread = jnp.concatenate([spread] * (piece // 128), axis=1)
    copies = []
    for n in range(pieces):
        at = pl.ds(n * piece, piece)
        value = raw[:, at]
        if n * piece < edge:
            value = value + from_down[:, at].astype(jnp.float32)
        if (n + 1) * piece > cells - edge:
            begin = n * piece - (cells - edge)
            value = value + from_up[:, pl.ds(begin, piece)].astype(jnp.float32)
        staged[:, at] = value / target[:, at] + spread
        copies.append(pltpu.make_async_copy(staged.at[:, at], out_hbm.at[:, at], sems.at[n]))
        copies[n].start()
    for copy in copies:
        copy.wait()


def total_over(values, axis):
    size = lax.axis_size(axis)
    if size & (size - 1) or size > 8:
        return lax.psum(values, axis)
    terms = [values]
    for step in range(1, size):
        terms.append(lax.ppermute(values, axis, [(i, i ^ step) for i in range(size)]))
    while len(terms) > 1:
        terms = [a + b for a, b in zip(terms[0::2], terms[1::2])]
    return terms[0]


def regrid(
    surface_fields, land_mask, source_area, target_area, weight_tiles, tile_of, block_of, live_slots
):
    members, fields, snapshots, cells = surface_fields.shape
    columns = members * fields * snapshots
    tile_count, tile, _ = weight_tiles.shape
    tgt_count, slots = tile_of.shape
    own_blocks = cells // tile
    stride = own_blocks // tgt_count
    edge = -(-HALO_BLK // stride)
    size = lax.axis_size("band")
    up = [(i, i + 1) for i in range(size - 1)]
    down = [(i + 1, i) for i in range(size - 1)]
    f32 = jnp.float32

    blank = tile_count << PLACE_BITS
    at_edge, edge_size = list_sizes(edge, slots)
    at_own, own_size = list_sizes(tgt_count, slots)
    tables = (tile_of.T, block_of.T, live_slots)
    low, high = pl.pallas_call(
        functools.partial(edge_body, own_blocks, blank, edge),
        out_shape=(jax.ShapeDtypeStruct((1, edge_size), jnp.int32),) * 2,
        in_specs=[SMEM] * 3,
        out_specs=(SMEM, SMEM),
        compiler_params=params(8),
        name="edges",
    )(*tables)
    up_list = lax.ppermute(low, "band", down)
    down_list = lax.ppermute(high, "band", up)

    weighted, tiles, totals, items = pl.pallas_call(
        weigh_body,
        out_shape=(
            jax.ShapeDtypeStruct((columns, cells), jnp.bfloat16),
            jax.ShapeDtypeStruct((tile_count + 1, tile, tile), jnp.bfloat16),
            jax.ShapeDtypeStruct((8, columns), f32),
            jax.ShapeDtypeStruct((1, own_size), jnp.int32),
        ),
        in_specs=[ANY, VMEM, VMEM, VMEM, ANY, SMEM, SMEM, SMEM],
        out_specs=(VMEM, VMEM, VMEM, SMEM),
        scratch_shapes=[
            pltpu.VMEM((columns, cells), jnp.bfloat16),
            pltpu.SemaphoreType.DMA((PIECES + 1,)),
        ],
        compiler_params=params(16),
        name="weigh",
    )(
        pltpu.with_memory_space_constraint(surface_fields.reshape(columns, cells), pltpu.HBM),
        land_mask.reshape(1, cells),
        source_area.reshape(1, cells),
        target_area.reshape(1, tgt_count * tile),
        pltpu.with_memory_space_constraint(weight_tiles, pltpu.HBM),
        *tables,
    )
    totals = total_over(totals, "band")

    to_up, to_down, reach_sums = pl.pallas_call(
        functools.partial(reach_body, at_edge),
        out_shape=(
            jax.ShapeDtypeStruct((columns, edge * tile), jnp.bfloat16),
            jax.ShapeDtypeStruct((columns, edge * tile), jnp.bfloat16),
            jax.ShapeDtypeStruct((8, columns), f32),
        ),
        in_specs=[SMEM, SMEM, VMEM, VMEM],
        out_specs=(VMEM, VMEM, VMEM),
        scratch_shapes=[pltpu.VMEM((columns, edge * tile), f32)] * 2,
        compiler_params=params(8),
        name="reach",
    )(up_list, down_list, weighted, tiles)
    from_down = lax.ppermute(to_up, "band", up)
    from_up = lax.ppermute(to_down, "band", down)

    raw, sums = pl.pallas_call(
        functools.partial(local_body, at_own),
        out_shape=(
            jax.ShapeDtypeStruct((columns, tgt_count * tile), f32),
            jax.ShapeDtypeStruct((8, columns), f32),
        ),
        in_specs=[SMEM, VMEM, VMEM, VMEM],
        out_specs=(VMEM, VMEM),
        compiler_params=params(8),
        name="local",
    )(items, weighted, tiles, reach_sums)
    sums = total_over(sums, "band")

    piece_count = 2 * tgt_count // edge
    regridded = pl.pallas_call(
        finish_body,
        out_shape=jax.ShapeDtypeStruct((columns, tgt_count * tile), f32),
        in_specs=[VMEM] * 6,
        out_specs=ANY,
        scratch_shapes=[
            pltpu.VMEM((columns, tgt_count * tile), f32),
            pltpu.SemaphoreType.DMA((piece_count,)),
        ],
        compiler_params=params(16),
        name="finish",
    )(raw, from_down, from_up, target_area.reshape(1, tgt_count * tile), totals, sums)

    conserved = (totals[0] / totals[1]).reshape(members, fields, snapshots)
    ensemble = total_over(jnp.sum(conserved, axis=0), "mem") / MEMBERS
    return regridded.reshape(members, fields, snapshots, tgt_count * tile), conserved, ensemble


def solution(mesh):
    placed = (
        P(("grp", "mem"), "fld", None, "band"),
        P("band"),
        P("band"),
        P("band"),
        P(),
        P("band", None),
        P("band", None),
        P("band"),
    )
    return jax.shard_map(
        regrid,
        mesh=mesh,
        in_specs=placed,
        out_specs=(
            P(("grp", "mem"), "fld", None, "band"),
            P(("grp", "mem"), "fld", None),
            P(("grp", "fld"), None),
        ),
        check_vma=False,
    )
```

time: 306 us -> 58.6 us (0.19)
  local copies, waits for them, and re-layouts: 128 us -> 4.56 us
  matrix products: 91.6 us -> 0 us
  other arithmetic: 35.9 us -> 0.63 us
  starting transfers between devices: 6.3 us -> 26.9 us
  Pallas kernels: 0 us -> 17.6 us
  waiting for transfers between devices: 24.5 us -> 7.65 us
  blocking collectives: 15.5 us -> 0 us
    gather x48 -> x0, local copies, waits for them, and re-layouts: 103 us -> none  [the longest x24 84.8 us: one_slot(): chosen = jnp.take(source, picked[:, position], axis=1)]
    dot_general x24 -> x0, matrix products: 91.6 us -> none  [one_slot(): jnp.einsum('cnb,nbd->cnd', chosen, weights, preferred_element_type=jnp.fl...]
    ppermute x2 -> x11, starting transfers between devices: 6.3 us -> 26.9 us  [the longest x7 16.3 us: total_over(): lax.ppermute(values, axis, [(i, i ^ step) for i in range(size)])]
    pallas_call x0 -> x5, Pallas kernels: none -> 17.6 us  [the longest x1 6.31 us: regrid(): pl.pallas_call(weigh_body, out_shape=(jax.ShapeDtypeStruct((columns, cell...]
    reduce_and x24 -> x0, other arithmetic: 17.1 us -> none  [one_slot(): chosen = jnp.take(source, picked[:, position], axis=1)]
    ppermute x2 -> x11, waiting for transfers between devices: 24.5 us -> 7.65 us  [the longest x1 4.42 us: regrid(): from_up = lax.ppermute(to_down, 'band', down)]
    psum x2 -> x0, blocking collectives: 15.5 us -> none  [the longest x1 10.5 us: band_totals(): return lax.psum((own_total, target_part, area_part), 'band')]
    concatenate x1 -> x0, local copies, waits for them, and re-layouts: 8.62 us -> none  [extended_2(): array = jnp.concatenate([before, array, after], axis=dim)]
  transfers between devices with their start and end apart: 2 -> 11, of which waited for: 2 -> 3; matrix products, arithmetic and copies ran while one was open for 0% -> 1% of each run, Pallas kernels for 0% -> 17%
where the time goes in v1:
time: 58.6 us; the launch traced here: 58.1 us
  starting transfers between devices  26.9 us (46%)
  Pallas kernels  17.6 us (30%)
  waiting for transfers between devices  7.65 us (13%)
  local copies, waits for them, and re-layouts  4.56 us (8%)
  between operations  0.76 us (1%)
  other arithmetic  0.63 us (1%)
    ppermute x7, starting transfers between devices, total_over(): lax.ppermute(values, axis, [(i, i ^ step) for i in range(size)])  16.3 us
    pallas_call x1, Pallas kernels, regrid(): pl.pallas_call(weigh_body, out_shape=(jax.ShapeDtypeStruct((columns, cell...  6.31 us
    pallas_call x1, Pallas kernels, regrid(): pl.pallas_call(functools.partial(local_body, at_own), out_shape=(jax.Shap...  5.53 us
    ppermute x1, starting transfers between devices, regrid(): down_list = lax.ppermute(high, 'band', up)  4.55 us
    unnamed x16, local copies, waits for them, and re-layouts  4.47 us
    ppermute x1, waiting for transfers between devices, regrid(): from_up = lax.ppermute(to_down, 'band', down)  4.42 us
    ppermute x1, starting transfers between devices, regrid(): from_down = lax.ppermute(to_up, 'band', up)  3.45 us
    pallas_call x1, Pallas kernels, regrid(): pl.pallas_call(functools.partial(edge_body, own_blocks, blank, edge), out...  3.16 us
  transfers between devices with their start and end apart: 11, of which 3 were waited for; matrix products, arithmetic and copies ran while one was open for 1% of the time, Pallas kernels for 17%

profile of v1, /device:TPU:0, one launch (start us, length us, event | category | flops | bytes accessed | tf_op | source)
XLA Modules:
  0.0 58.1 jit_solution(14279841038378099419)
XLA Ops:
  0.6 0.0 copy-start
  0.6 0.8 %copy-done = s32[16384]{0:T(1024)S(1)} copy-done((s32[16384]{0:T(1024)S(1)}, s32[16384]{0:T(1024)}, u32[]{:S(2)}) %copy-start) | copy-done | bytes 65560
  1.5 0.0 copy-start.1
  1.5 0.8 %copy-done.1 = f32[16384]{0:T(1024)S(1)} copy-done((f32[16384]{0:T(1024)S(1)}, f32[16384]{0:T(1024)}, u32[]{:S(2)}) %copy-start.1) | copy-done | bytes 65560
  2.3 0.0 copy-start.2
  2.3 0.7 %copy-done.2 = f32[4096]{0:T(1024)S(1)} copy-done((f32[4096]{0:T(1024)S(1)}, f32[4096]{0:T(1024)}, u32[]{:S(2)}) %copy-start.2) | copy-done | bytes 16408
  3.0 0.0 copy-start.4
  3.0 0.7 %copy-done.4 = s32[32,24]{0,1:T(8,128)S(1)} copy-done((s32[32,24]{0,1:T(8,128)S(1)}, s32[32,24]{0,1:T(8,128)}, u32[]{:S(2)}) %copy-start.4) | copy-done | bytes 3096
  3.7 0.0 copy-start.5
  3.7 0.7 %copy-done.5 = s32[32,24]{0,1:T(8,128)S(1)} copy-done((s32[32,24]{0,1:T(8,128)S(1)}, s32[32,24]{0,1:T(8,128)}, u32[]{:S(2)}) %copy-start.5) | copy-done | bytes 3096
  4.4 0.0 copy-start.6
  4.4 0.7 %copy-done.6 = s32[32]{0:T(128)S(1)} copy-done((s32[32]{0:T(128)S(1)}, s32[32]{0:T(128)}, u32[]{:S(2)}) %copy-start.6) | copy-done | bytes 152
  5.1 6.3 %weigh.1 = (bf16[128,16384]{1,0:T(8,128)(2,1)S(1)}, bf16[17,128,128]{2,1,0:T(8,128)(2,1)S(1)}, f32[8,128]{1,0:T(8,128)S(1)}, s32[1,1024]{1,0:T(1,128)S(1)}) custom-call(bf16[128,16384]{1,0:T(8,128)(2,1)} %bitcast.15, s32[1,16384]{1,0:T(1,128)S(1)} %bitcast.7, f32[1,16384]{1,0:T(1,128)S(1)} %bitcast.8, f32[1,4096]{1,0:T(1,128)S(1)} %bitcast.9, ...), custom_call_target="tpu_custom_call" | custom-call | tf_op jit(solution)/shard_map/weigh/pallas_call | solution.py:243
  11.4 3.8 %collective-permute-start.5 = (f32[8,128]{1,0:T(8,128)S(1)}, f32[8,128]{1,0:T(8,128)S(1)}, u32[]{:S(2)}, u32[]{:S(2)}) collective-permute-start(f32[8,128]{1,0:T(8,128)S(1)} %get-tuple-element.23), channel_id=1, source_target_pairs={{0,8},{4,12},{8,0},{12,4},{1,9},{5,13},{9,1},{13,5},{2,10},{6,14},... | collective-permute-start | bytes 12296 | tf_op jit(solution)/shard_map/ppermute | solution.py:207
  15.2 3.4 %collective-permute-start.6 = (f32[8,128]{1,0:T(8,128)S(1)}, f32[8,128]{1,0:T(8,128)S(1)}, u32[]{:S(2)}, u32[]{:S(2)}) collective-permute-start(f32[8,128]{1,0:T(8,128)S(1)} %get-tuple-element.23), channel_id=1, source_target_pairs={{0,12},{4,8},{8,4},{12,0},{1,13},{5,9},{9,5},{13,1},{2,14},{6,10},... | collective-permute-start | bytes 12296 | tf_op jit(solution)/shard_map/ppermute | solution.py:207
  18.6 0.5 collective-permute-start.4
  19.1 3.2 %edges.1 = (s32[1,384]{1,0:T(1,128)S(1)}, s32[1,384]{1,0:T(1,128)S(1)}) custom-call(s32[24,32]{1,0:T(8,128)S(1)} %bitcast.12, s32[24,32]{1,0:T(8,128)S(1)} %bitcast.14, s32[32]{0:T(128)S(1)} %copy-done.6), custom_call_target="tpu_custom_call" | custom-call | tf_op jit(solution)/shard_map/edges/pallas_call | solution.py:232
  22.3 1.3 %collective-permute-start = (s32[1,384]{1,0:T(1,128)S(1)}, s32[1,384]{1,0:T(1,128)S(1)}, u32[]{:S(2)}, u32[]{:S(2)}) collective-permute-start(s32[1,384]{1,0:T(1,128)S(1)} %get-tuple-element.17), channel_id=1, source_target_pairs={{4,0},{8,4},{12,8},{5,1},{9,5},{13,9},{6,2},{10,6},{14,10},{7,3},{... | collective-permute-start | bytes 4616 | tf_op jit(solution)/shard_map/ppermute | solution.py:240
  23.6 4.5 %collective-permute-start.1 = (s32[1,384]{1,0:T(1,128)S(1)}, s32[1,384]{1,0:T(1,128)S(1)}, u32[]{:S(2)}, u32[]{:S(2)}) collective-permute-start(s32[1,384]{1,0:T(1,128)S(1)} %get-tuple-element.18), channel_id=1, source_target_pairs={{0,4},{4,8},{8,12},{1,5},{5,9},{9,13},{2,6},{6,10},{10,14},{3,7},{... | collective-permute-start | bytes 4616 | tf_op jit(solution)/shard_map/ppermute | solution.py:241
  28.1 0.0 collective-permute-done.up_items
  28.1 1.3 %collective-permute-done.1.down_items = s32[1,384]{1,0:T(1,128)S(1)} collective-permute-done((s32[1,384]{1,0:T(1,128)S(1)}, s32[1,384]{1,0:T(1,128)S(1)}, u32[]{:S(2)}, u32[]{:S(2)}) %collective-permute-start.1) | collective-permute-done | bytes 1568 | tf_op jit(solution)/shard_map/ppermute | solution.py:241
  29.4 0.0 copy-start.3
  29.4 1.1 %reach.1 = (bf16[128,1024]{1,0:T(8,128)(2,1)S(1)}, bf16[128,1024]{1,0:T(8,128)(2,1)S(1)}, f32[8,128]{1,0:T(8,128)S(1)}) custom-call(s32[1,384]{1,0:T(1,128)S(1)} %collective-permute-done.up_items, s32[1,384]{1,0:T(1,128)S(1)} %collective-permute-done.1.down_items, bf16[128,16384]{1,0:T(8,128)(2,1)S(1)} %get-tuple-element.15.weighted, ...), custom_call_target="tpu_custom_call" | custom-call | tf_op jit(solution)/shard_map/reach/pallas_call | solution.py:269
  30.5 5.5 %local.1 = (f32[128,4096]{1,0:T(8,128)S(1)}, f32[8,128]{1,0:T(8,128)S(1)}) custom-call(s32[1,1024]{1,0:T(1,128)S(1)} %get-tuple-element.14.items, bf16[128,16384]{1,0:T(8,128)(2,1)S(1)} %get-tuple-element.15.weighted, bf16[17,128,128]{2,1,0:T(8,128)(2,1)S(1)} %get-tuple-element.16.tiles, f32[8,128]{1,0:T(8,128)S(1)} %get-tuple-element.19.reach_sums), custom_call_target="tpu_custom_call" | custom-call | tf_op jit(solution)/shard_map/local/pallas_call | solution.py:285
  36.1 3.6 %collective-permute-start.8 = (f32[8,128]{1,0:T(8,128)S(1)}, f32[8,128]{1,0:T(8,128)S(1)}, u32[]{:S(2)}, u32[]{:S(2)}) collective-permute-start(f32[8,128]{1,0:T(8,128)S(1)} %get-tuple-element.24), channel_id=1, source_target_pairs={{0,8},{4,12},{8,0},{12,4},{1,9},{5,13},{9,1},{13,5},{2,10},{6,14},... | collective-permute-start | bytes 12296 | tf_op jit(solution)/shard_map/ppermute | solution.py:207
  39.7 3.0 %collective-permute-start.9 = (f32[8,128]{1,0:T(8,128)S(1)}, f32[8,128]{1,0:T(8,128)S(1)}, u32[]{:S(2)}, u32[]{:S(2)}) collective-permute-start(f32[8,128]{1,0:T(8,128)S(1)} %get-tuple-element.24), channel_id=1, source_target_pairs={{0,12},{4,8},{8,4},{12,0},{1,13},{5,9},{9,5},{13,1},{2,14},{6,10},... | collective-permute-start | bytes 12296 | tf_op jit(solution)/shard_map/ppermute | solution.py:207
  42.7 0.0 collective-permute-done.5
  42.7 0.5 collective-permute-start.7
  43.1 0.0 collective-permute-done.6
  43.2 0.0 collective-permute-done.4
  43.2 0.1 div.18
  43.3 0.0 copy-start.7
  43.3 1.6 %collective-permute-start.10 = (f32[4,8]{1,0:T(4,128)S(1)}, f32[4,8]{1,0:T(4,128)S(1)}, u32[]{:S(2)}, u32[]{:S(2)}) collective-permute-start(f32[4,8]{1,0:T(4,128)S(1)} %reduce_sum.9), channel_id=1, source_target_pairs={{0,2},{2,0},{1,3},{3,1},{4,6},{6,4},{5,7},{7,5},{8,10},{10,8},{9,1... | collective-permute-start | bytes 392 | tf_op jit(solution)/shard_map/ppermute | solution.py:207
  44.9 3.4 %collective-permute-start.2 = (bf16[128,1024]{1,0:T(8,128)(2,1)S(1)}, bf16[128,1024]{1,0:T(8,128)(2,1)S(1)}, u32[]{:S(2)}, u32[]{:S(2)}) collective-permute-start(bf16[128,1024]{1,0:T(8,128)(2,1)S(1)} %get-tuple-element.21), channel_id=1, source_target_pairs={{0,4},{4,8},{8,12},{1,5},{5,9},{9,13},{2,6},{6,10},{10,14},{3,7},{... | collective-permute-start | bytes 786440 | tf_op jit(solution)/shard_map/ppermute | solution.py:282
  48.3 0.0 collective-permute-done.10
  48.3 1.3 %collective-permute-start.3 = (bf16[128,1024]{1,0:T(8,128)(2,1)S(1)}, bf16[128,1024]{1,0:T(8,128)(2,1)S(1)}, u32[]{:S(2)}, u32[]{:S(2)}) collective-permute-start(bf16[128,1024]{1,0:T(8,128)(2,1)S(1)} %get-tuple-element.22), channel_id=1, source_target_pairs={{4,0},{8,4},{12,8},{5,1},{9,5},{13,9},{6,2},{10,6},{14,10},{7,3},{... | collective-permute-start | bytes 786440 | tf_op jit(solution)/shard_map/ppermute | solution.py:283
  49.6 0.6 %add_multiply_fusion = f32[4,8]{1,0:T(4,128)} fusion(f32[4,8]{1,0:T(4,128)S(1)} %reduce_sum.9, f32[4,8]{1,0:T(4,128)S(1)} %collective-permute-done.10), kind=kLoop, calls=%fused_computation.2 | loop fusion | flops 64 | bytes 384 | tf_op jit(solution)/shard_map/div | solution.py:313
  50.2 0.0 collective-permute-done.8
  50.2 0.0 collective-permute-done.9
  50.2 0.0 collective-permute-done.7
  50.2 1.9 %collective-permute-done.2.from_down = bf16[128,1024]{1,0:T(8,128)(2,1)S(1)} collective-permute-done((bf16[128,1024]{1,0:T(8,128)(2,1)S(1)}, bf16[128,1024]{1,0:T(8,128)(2,1)S(1)}, u32[]{:S(2)}, u32[]{:S(2)}) %collective-permute-start.2) | collective-permute-done | bytes 262176 | tf_op jit(solution)/shard_map/ppermute | solution.py:282
  52.2 4.4 %collective-permute-done.3.from_up = bf16[128,1024]{1,0:T(8,128)(2,1)S(1)} collective-permute-done((bf16[128,1024]{1,0:T(8,128)(2,1)S(1)}, bf16[128,1024]{1,0:T(8,128)(2,1)S(1)}, u32[]{:S(2)}, u32[]{:S(2)}) %collective-permute-start.3) | collective-permute-done | bytes 262176 | tf_op jit(solution)/shard_map/ppermute | solution.py:283
  56.6 0.0 copy-done.3
  56.6 1.5 %finish.1 = f32[128,4096]{1,0:T(8,128)} custom-call(f32[128,4096]{1,0:T(8,128)S(1)} %get-tuple-element.20.raw, bf16[128,1024]{1,0:T(8,128)(2,1)S(1)} %collective-permute-done.2.from_down, bf16[128,1024]{1,0:T(8,128)(2,1)S(1)} %collective-permute-done.3.from_up, f32[1,4096]{1,0:T(1,128)S(1)} %bitcast.10, f32[8,128]{1,0:T(8,128)S(1)} %add_add_fusion.1.totals, ...), custom_call_target="tpu_custom_call" | custom-call | tf_op jit(solution)/shard_map/finish/pallas_call | solution.py:299
  58.1 0.0 copy-done.7
  (4 shorter events, 0.1 us)
Async XLA Ops:
  0.6 0.8 %copy-start = (s32[16384]{0:T(1024)S(1)}, s32[16384]{0:T(1024)}, u32[]{:S(2)}) copy-start(s32[16384]{0:T(1024)} %param.9) | copy-start | bytes 196612
  1.5 0.8 %copy-start.1 = (f32[16384]{0:T(1024)S(1)}, f32[16384]{0:T(1024)}, u32[]{:S(2)}) copy-start(f32[16384]{0:T(1024)} %param.10) | copy-start | bytes 196612
  2.3 0.7 %copy-start.2 = (f32[4096]{0:T(1024)S(1)}, f32[4096]{0:T(1024)}, u32[]{:S(2)}) copy-start(f32[4096]{0:T(1024)} %param.11) | copy-start | bytes 49156
  3.0 0.7 %copy-start.4 = (s32[32,24]{0,1:T(8,128)S(1)}, s32[32,24]{0,1:T(8,128)}, u32[]{:S(2)}) copy-start(s32[32,24]{0,1:T(8,128)} %param.13) | copy-start | bytes 9220
  3.7 0.7 %copy-start.5 = (s32[32,24]{0,1:T(8,128)S(1)}, s32[32,24]{0,1:T(8,128)}, u32[]{:S(2)}) copy-start(s32[32,24]{0,1:T(8,128)} %param.14) | copy-start | bytes 9220
  4.4 0.7 %copy-start.6 = (s32[32]{0:T(128)S(1)}, s32[32]{0:T(128)}, u32[]{:S(2)}) copy-start(s32[32]{0:T(128)} %live.3) | copy-start | bytes 388
  11.4 31.2 %collective-permute-start.5 = (f32[8,128]{1,0:T(8,128)S(1)}, f32[8,128]{1,0:T(8,128)S(1)}, u32[]{:S(2)}, u32[]{:S(2)}) collective-permute-start(f32[8,128]{1,0:T(8,128)S(1)} %get-tuple-element.23), channel_id=1, source_target_pairs={{0,8},{4,12},{8,0},{12,4},{1,9},{5,13},{9,1},{13,5},{2,10},{6,14},... | collective-permute-start | bytes 12296 | tf_op jit(solution)/shard_map/ppermute | solution.py:207
  15.2 27.9 %collective-permute-start.6 = (f32[8,128]{1,0:T(8,128)S(1)}, f32[8,128]{1,0:T(8,128)S(1)}, u32[]{:S(2)}, u32[]{:S(2)}) collective-permute-start(f32[8,128]{1,0:T(8,128)S(1)} %get-tuple-element.23), channel_id=1, source_target_pairs={{0,12},{4,8},{8,4},{12,0},{1,13},{5,9},{9,5},{13,1},{2,14},{6,10},... | collective-permute-start | bytes 12296 | tf_op jit(solution)/shard_map/ppermute | solution.py:207
  18.6 24.5 %collective-permute-start.4 = (f32[8,128]{1,0:T(8,128)S(1)}, f32[8,128]{1,0:T(8,128)S(1)}, u32[]{:S(2)}, u32[]{:S(2)}) collective-permute-start(f32[8,128]{1,0:T(8,128)S(1)} %get-tuple-element.23), channel_id=1, source_target_pairs={{0,4},{4,0},{8,12},{12,8},{1,5},{5,1},{9,13},{13,9},{2,6},{6,2},{1... | collective-permute-start | bytes 12296 | tf_op jit(solution)/shard_map/ppermute | solution.py:207
  22.3 5.9 %collective-permute-start = (s32[1,384]{1,0:T(1,128)S(1)}, s32[1,384]{1,0:T(1,128)S(1)}, u32[]{:S(2)}, u32[]{:S(2)}) collective-permute-start(s32[1,384]{1,0:T(1,128)S(1)} %get-tuple-element.17), channel_id=1, source_target_pairs={{4,0},{8,4},{12,8},{5,1},{9,5},{13,9},{6,2},{10,6},{14,10},{7,3},{... | collective-permute-start | bytes 4616 | tf_op jit(solution)/shard_map/ppermute | solution.py:240
  23.6 5.8 %collective-permute-start.1 = (s32[1,384]{1,0:T(1,128)S(1)}, s32[1,384]{1,0:T(1,128)S(1)}, u32[]{:S(2)}, u32[]{:S(2)}) collective-permute-start(s32[1,384]{1,0:T(1,128)S(1)} %get-tuple-element.18), channel_id=1, source_target_pairs={{0,4},{4,8},{8,12},{1,5},{5,9},{9,13},{2,6},{6,10},{10,14},{3,7},{... | collective-permute-start | bytes 4616 | tf_op jit(solution)/shard_map/ppermute | solution.py:241
  29.4 27.2 %copy-start.3 = (f32[4096]{0:T(1024)S(1)}, f32[4096]{0:T(1024)}, u32[]{:S(2)}) copy-start(f32[4096]{0:T(1024)} %param.11) | copy-start | bytes 49156
  36.1 14.2 %collective-permute-start.8 = (f32[8,128]{1,0:T(8,128)S(1)}, f32[8,128]{1,0:T(8,128)S(1)}, u32[]{:S(2)}, u32[]{:S(2)}) collective-permute-start(f32[8,128]{1,0:T(8,128)S(1)} %get-tuple-element.24), channel_id=1, source_target_pairs={{0,8},{4,12},{8,0},{12,4},{1,9},{5,13},{9,1},{13,5},{2,10},{6,14},... | collective-permute-start | bytes 12296 | tf_op jit(solution)/shard_map/ppermute | solution.py:207
  39.7 10.6 %collective-permute-start.9 = (f32[8,128]{1,0:T(8,128)S(1)}, f32[8,128]{1,0:T(8,128)S(1)}, u32[]{:S(2)}, u32[]{:S(2)}) collective-permute-start(f32[8,128]{1,0:T(8,128)S(1)} %get-tuple-element.24), channel_id=1, source_target_pairs={{0,12},{4,8},{8,4},{12,0},{1,13},{5,9},{9,5},{13,1},{2,14},{6,10},... | collective-permute-start | bytes 12296 | tf_op jit(solution)/shard_map/ppermute | solution.py:207
  42.7 7.6 %collective-permute-start.7 = (f32[8,128]{1,0:T(8,128)S(1)}, f32[8,128]{1,0:T(8,128)S(1)}, u32[]{:S(2)}, u32[]{:S(2)}) collective-permute-start(f32[8,128]{1,0:T(8,128)S(1)} %get-tuple-element.24), channel_id=1, source_target_pairs={{0,4},{4,0},{8,12},{12,8},{1,5},{5,1},{9,13},{13,9},{2,6},{6,2},{1... | collective-permute-start | bytes 12296 | tf_op jit(solution)/shard_map/ppermute | solution.py:207
  43.3 14.9 %copy-start.7 = (f32[4,4,8]{2,1,0:T(4,128)}, f32[4,4,8]{2,1,0:T(4,128)S(1)}, u32[]{:S(2)}) copy-start(f32[4,4,8]{2,1,0:T(4,128)S(1)} %div.18) | copy-start | bytes 1540
  43.3 5.0 %collective-permute-start.10 = (f32[4,8]{1,0:T(4,128)S(1)}, f32[4,8]{1,0:T(4,128)S(1)}, u32[]{:S(2)}, u32[]{:S(2)}) collective-permute-start(f32[4,8]{1,0:T(4,128)S(1)} %reduce_sum.9), channel_id=1, source_target_pairs={{0,2},{2,0},{1,3},{3,1},{4,6},{6,4},{5,7},{7,5},{8,10},{10,8},{9,1... | collective-permute-start | bytes 392 | tf_op jit(solution)/shard_map/ppermute | solution.py:207
  44.9 7.3 %collective-permute-start.2 = (bf16[128,1024]{1,0:T(8,128)(2,1)S(1)}, bf16[128,1024]{1,0:T(8,128)(2,1)S(1)}, u32[]{:S(2)}, u32[]{:S(2)}) collective-permute-start(bf16[128,1024]{1,0:T(8,128)(2,1)S(1)} %get-tuple-element.21), channel_id=1, source_target_pairs={{0,4},{4,8},{8,12},{1,5},{5,9},{9,13},{2,6},{6,10},{10,14},{3,7},{... | collective-permute-start | bytes 786440 | tf_op jit(solution)/shard_map/ppermute | solution.py:282
  48.3 8.3 %collective-permute-start.3 = (bf16[128,1024]{1,0:T(8,128)(2,1)S(1)}, bf16[128,1024]{1,0:T(8,128)(2,1)S(1)}, u32[]{:S(2)}, u32[]{:S(2)}) collective-permute-start(bf16[128,1024]{1,0:T(8,128)(2,1)S(1)} %get-tuple-element.22), channel_id=1, source_target_pairs={{4,0},{8,4},{12,8},{5,1},{9,5},{13,9},{6,2},{10,6},{14,10},{7,3},{... | collective-permute-start | bytes 786440 | tf_op jit(solution)/shard_map/ppermute | solution.py:283

commit v2 on v1

v2 whole, which is shorter than its diff:
```python
import functools

import jax
import jax.numpy as jnp
from jax import lax
from jax.experimental import pallas as pl
from jax.experimental.pallas import tpu as pltpu
from jax.sharding import PartitionSpec as P


MEMBERS = 8
HALO_BLK = 32
CHUNK = 4
CHUNK_BITS = 2
UNROLL = 4
UNROLL_BITS = 2
PIECES = 8
PLACE_BITS = 16

VMEM = pl.BlockSpec(memory_space=pltpu.VMEM)
SMEM = pl.BlockSpec(memory_space=pltpu.SMEM)
ANY = pl.BlockSpec(memory_space=pl.ANY)


def params(mib):
    return pltpu.CompilerParams(vmem_limit_bytes=mib * 1024 * 1024)


def row_of(acc):
    return jnp.sum(acc.T, axis=0, keepdims=True)


def packed(mask, code, blank):
    slots, targets = code.shape
    ones = jnp.where(mask, 1.0, 0.0)
    above = lax.broadcasted_iota(jnp.int32, (slots, slots), 0)
    below = lax.broadcasted_iota(jnp.int32, (slots, slots), 1)
    before = jnp.where(below < above, 1.0, 0.0).astype(jnp.bfloat16)
    rank = jnp.dot(before, ones.astype(jnp.bfloat16), preferred_element_type=jnp.float32)
    rank = jnp.where(mask, rank, -1.0).astype(jnp.int32)
    extra = (code - blank).astype(jnp.float32)
    rows = [
        jnp.sum(jnp.where(rank == p, extra, 0.0), axis=0, keepdims=True) for p in range(slots)
    ]
    body = jnp.concatenate(rows, axis=0).astype(jnp.int32) + blank
    counts = jnp.sum(ones, axis=0, keepdims=True).astype(jnp.int32)
    row = lax.broadcasted_iota(jnp.int32, (8, targets), 0)
    return jnp.concatenate([body, jnp.where(row == 0, counts, blank)], axis=0)


def edge_body(own_blocks, blank, tile_hbm, block_hbm, live_hbm, own, low, high, tiles, blocks, live, sems):
    copies = [
        pltpu.make_async_copy(source, place, sems.at[n])
        for n, (source, place) in enumerate(((tile_hbm, tiles), (block_hbm, blocks), (live_hbm, live)))
    ]
    for copy in copies:
        copy.start()
    for copy in copies:
        copy.wait()
    band = lax.axis_index("band")
    slot = lax.broadcasted_iota(jnp.int32, tiles.shape, 0)
    alive = slot < live[...]
    block = blocks[...] - HALO_BLK
    code = (tiles[...] << PLACE_BITS) + block
    below = jnp.where(band > 0, 0, -HALO_BLK)
    above = jnp.where(band < lax.axis_size("band") - 1, own_blocks, own_blocks + HALO_BLK)
    low[...] = packed(alive & (block < below), code + own_blocks, blank)
    high[...] = packed(alive & (block >= above), code - own_blocks, blank)
    own[...] = packed(alive & (block >= 0) & (block < own_blocks), code, blank)


def weigh_body(
    fields_hbm, mask_hbm, area_hbm, target_hbm, tiles_hbm,
    weighted, totals, tiles, fields, mask, source, target, sems,
):
    columns, cells = weighted.shape
    tile_count, tile, lanes = tiles_hbm.shape
    step = 4 * tile
    piece = cells // PIECES
    small = [
        pltpu.make_async_copy(mask_hbm, mask, sems.at[PIECES]),
        pltpu.make_async_copy(area_hbm, source, sems.at[PIECES + 1]),
        pltpu.make_async_copy(target_hbm, target, sems.at[PIECES + 2]),
        pltpu.make_async_copy(tiles_hbm, tiles.at[pl.ds(0, tile_count)], sems.at[PIECES + 3]),
    ]
    copies = [
        pltpu.make_async_copy(
            fields_hbm.at[:, pl.ds(n * piece, piece)],
            fields.at[:, pl.ds(n * piece, piece)],
            sems.at[n],
        )
        for n in range(PIECES)
    ]
    for copy in small[:3] + copies + small[3:]:
        copy.start()
    tiles[tile_count] = jnp.zeros((tile, lanes), tiles.dtype)
    for copy in small[:3]:
        copy.wait()
    area = jnp.sum(target[...], axis=1, keepdims=True)
    acc = jnp.zeros((columns, tile), jnp.float32)
    for n in range(PIECES):
        copies[n].wait()

        def one(k, acc):
            at = pl.ds(pl.multiple_of(n * piece + k * step, step), step)
            factor = source[:, at] * mask[:, at].astype(jnp.float32)
            value = (factor * fields[:, at].astype(jnp.float32)).astype(jnp.bfloat16)
            weighted[:, at] = value
            wide = value.astype(jnp.float32)
            for q in range(4):
                acc = acc + wide[:, q * tile : (q + 1) * tile]
            return acc

        acc = lax.fori_loop(0, piece // step, one, acc)
    own = row_of(acc)
    rows = lax.broadcasted_iota(jnp.int32, (8, columns), 0)
    totals[...] = jnp.where(rows == 0, own, jnp.where(rows == 1, area, 0.0))
    small[3].wait()


def run_items(codes, first, weighted, tiles, out, work):
    tile = tiles.shape[1]
    slots = codes.shape[0] - 8
    chunks = slots // CHUNK
    out[...] = jnp.zeros(out.shape, out.dtype)

    def one_target(n, items):
        for q in range(chunks):
            work[items + q] = (q << PLACE_BITS) + n
        return items + ((codes[slots, first + n] + CHUNK - 1) >> CHUNK_BITS)

    count = lax.fori_loop(0, out.shape[1] // tile, one_target, 0)
    for q in range(UNROLL):
        work[count + q] = (slots + 4) // CHUNK << PLACE_BITS

    def one(step, nothing):
        products = []
        for u in range(UNROLL):
            item = work[step * UNROLL + u]
            row = (item >> PLACE_BITS) * CHUNK
            column = first + (item & ((1 << PLACE_BITS) - 1))
            left, right = [], []
            for q in range(CHUNK):
                code = codes[row + q, column]
                block = code & ((1 << PLACE_BITS) - 1)
                left.append(weighted[:, pl.ds(pl.multiple_of(block * tile, tile), tile)])
                right.append(tiles[code >> PLACE_BITS])
            products.append(
                jnp.dot(
                    jnp.concatenate(left, axis=1),
                    jnp.concatenate(right, axis=0),
                    preferred_element_type=jnp.float32,
                )
            )
        for u in range(UNROLL):
            target = work[step * UNROLL + u] & ((1 << PLACE_BITS) - 1)
            place = pl.ds(pl.multiple_of(target * tile, tile), tile)
            out[:, place] = out[:, place] + products[u]
        return nothing

    lax.fori_loop(0, (count + UNROLL - 1) >> UNROLL_BITS, one, 0)
    acc = out[:, :tile]
    for n in range(1, out.shape[1] // tile):
        acc = acc + out[:, n * tile : (n + 1) * tile]
    return acc


def reach_body(up_codes, down_codes, weighted, tiles, to_up, to_down, sums, first, second, work):
    tile = tiles.shape[1]
    acc = run_items(up_codes, 0, weighted, tiles, first, work)
    start = down_codes.shape[1] - second.shape[1] // tile
    to_up[...] = first[...].astype(to_up.dtype)
    acc = acc + run_items(down_codes, start, weighted, tiles, second, work)
    to_down[...] = second[...].astype(to_down.dtype)
    sums[...] = jnp.broadcast_to(row_of(acc), sums.shape)


def local_body(codes, weighted, tiles, reach_sums, totals, peers, raw, sums, work):
    acc = run_items(codes, 0, weighted, tiles, raw, work)
    reached = reach_sums[0:1] + row_of(acc)
    rows = lax.broadcasted_iota(jnp.int32, sums.shape, 0)
    sums[...] = jnp.where(rows == 2, reached, jnp.where(rows == 3, peers[0:1], totals[...]))


def finish_body(raw, from_down, from_up, target, totals, out_hbm, staged, sems):
    columns, cells = raw.shape
    edge = from_down.shape[1]
    piece = edge // 2
    pieces = cells // piece
    correction = (totals[0:1] - totals[2:3]) / totals[1:2]
    spread = jnp.broadcast_to(correction, (128, columns)).T
    spread = jnp.concatenate([spread] * (piece // 128), axis=1)
    copies = []
    for n in range(pieces):
        at = pl.ds(n * piece, piece)
        value = raw[:, at]
        if n * piece < edge:
            value = value + from_down[:, at].astype(jnp.float32)
        if (n + 1) * piece > cells - edge:
            begin = n * piece - (cells - edge)
            value = value + from_up[:, pl.ds(begin, piece)].astype(jnp.float32)
        staged[:, at] = value / target[:, at] + spread
        copies.append(pltpu.make_async_copy(staged.at[:, at], out_hbm.at[:, at], sems.at[n]))
        copies[n].start()
    for copy in copies:
        copy.wait()


def total_over(values, axis):
    size = lax.axis_size(axis)
    if size & (size - 1):
        return lax.psum(values, axis)
    step = 1
    while step < size:
        values = values + lax.ppermute(values, axis, [(i, i ^ step) for i in range(size)])
        step *= 2
    return values


def regrid(
    surface_fields, land_mask, source_area, target_area, weight_tiles, tile_of, block_of, live_slots
):
    members, fields, snapshots, cells = surface_fields.shape
    columns = members * fields * snapshots
    tile_count, tile, _ = weight_tiles.shape
    tgt_count, slots = tile_of.shape
    own_blocks = cells // tile
    stride = own_blocks // tgt_count
    edge = -(-HALO_BLK // stride)
    size = lax.axis_size("band")
    up = [(i, (i + 1) % size) for i in range(size)]
    down = [(j, i) for i, j in up]
    f32 = jnp.float32
    blank = tile_count << PLACE_BITS
    work_size = slots // CHUNK
    listing = jax.ShapeDtypeStruct((slots + 8, tgt_count), jnp.int32)
    in_hbm = lambda x: pltpu.with_memory_space_constraint(x, pltpu.HBM)
    codes, low, high = pl.pallas_call(
        functools.partial(edge_body, own_blocks, blank),
        out_shape=(listing,) * 3,
        in_specs=[ANY] * 3,
        out_specs=(VMEM,) * 3,
        scratch_shapes=[
            pltpu.VMEM((slots, tgt_count), jnp.int32),
            pltpu.VMEM((slots, tgt_count), jnp.int32),
            pltpu.VMEM((1, tgt_count), jnp.int32),
            pltpu.SemaphoreType.DMA((3,)),
        ],
        compiler_params=params(4),
        name="edges",
    )(in_hbm(tile_of.T), in_hbm(block_of.T), in_hbm(live_slots.reshape(1, tgt_count)))
    up_codes = lax.ppermute(low, "band", down)
    down_codes = lax.ppermute(high, "band", up)

    weighted, totals, tiles = pl.pallas_call(
        weigh_body,
        out_shape=(
            jax.ShapeDtypeStruct((columns, cells), jnp.bfloat16),
            jax.ShapeDtypeStruct((8, columns), f32),
            jax.ShapeDtypeStruct((tile_count + 1, tile, tile), jnp.bfloat16),
        ),
        in_specs=[ANY] * 5,
        out_specs=(VMEM,) * 3,
        scratch_shapes=[
            pltpu.VMEM((columns, cells), jnp.bfloat16),
            pltpu.VMEM((1, cells), jnp.int32),
            pltpu.VMEM((1, cells), f32),
            pltpu.VMEM((1, tgt_count * tile), f32),
            pltpu.SemaphoreType.DMA((PIECES + 4,)),
        ],
        compiler_params=params(16),
        name="weigh",
    )(
        in_hbm(surface_fields.reshape(columns, cells)),
        in_hbm(land_mask.reshape(1, cells)),
        in_hbm(source_area.reshape(1, cells)),
        in_hbm(target_area.reshape(1, tgt_count * tile)),
        in_hbm(weight_tiles),
    )
    peers = total_over(totals, "mem")

    to_up, to_down, reach_sums = pl.pallas_call(
        reach_body,
        out_shape=(
            jax.ShapeDtypeStruct((columns, edge * tile), jnp.bfloat16),
            jax.ShapeDtypeStruct((columns, edge * tile), jnp.bfloat16),
            jax.ShapeDtypeStruct((8, columns), f32),
        ),
        in_specs=[SMEM, SMEM, VMEM, VMEM],
        out_specs=(VMEM, VMEM, VMEM),
        scratch_shapes=[pltpu.VMEM((columns, edge * tile), f32)] * 2
        + [pltpu.SMEM((edge * work_size + 8,), jnp.int32)],
        compiler_params=params(8),
        name="reach",
    )(up_codes, down_codes, weighted, tiles)
    from_down = lax.ppermute(to_up, "band", up)
    from_up = lax.ppermute(to_down, "band", down)

    raw, sums = pl.pallas_call(
        local_body,
        out_shape=(
            jax.ShapeDtypeStruct((columns, tgt_count * tile), f32),
            jax.ShapeDtypeStruct((8, columns), f32),
        ),
        in_specs=[SMEM, VMEM, VMEM, VMEM, VMEM, VMEM],
        out_specs=(VMEM, VMEM),
        scratch_shapes=[pltpu.SMEM((tgt_count * work_size + 8,), jnp.int32)],
        compiler_params=params(8),
        name="local",
    )(codes, weighted, tiles, reach_sums, totals, peers)
    totals = total_over(sums, "band")

    piece_count = 2 * tgt_count // edge
    regridded = pl.pallas_call(
        finish_body,
        out_shape=jax.ShapeDtypeStruct((columns, tgt_count * tile), f32),
        in_specs=[VMEM] * 5,
        out_specs=ANY,
        scratch_shapes=[
            pltpu.VMEM((columns, tgt_count * tile), f32),
            pltpu.SemaphoreType.DMA((piece_count,)),
        ],
        compiler_params=params(16),
        name="finish",
    )(raw, from_down, from_up, target_area.reshape(1, tgt_count * tile), totals)

    conserved = (totals[0] / totals[1]).reshape(members, fields, snapshots)
    ensemble = jnp.sum((totals[3] / totals[1]).reshape(members, fields, snapshots), axis=0) / MEMBERS
    return regridded.reshape(members, fields, snapshots, tgt_count * tile), conserved, ensemble


def solution(mesh):
    placed = (
        P(("grp", "mem"), "fld", None, "band"),
        P("band"),
        P("band"),
        P("band"),
        P(),
        P("band", None),
        P("band", None),
        P("band"),
    )
    return jax.shard_map(
        regrid,
        mesh=mesh,
        in_specs=placed,
        out_specs=(
            P(("grp", "mem"), "fld", None, "band"),
            P(("grp", "mem"), "fld", None),
            P(("grp", "fld"), None),
        ),
        check_vma=False,
    )
```

time: 58.6 us -> 45 us (0.77)
  starting transfers between devices: 26.9 us -> 12.3 us
  waiting for transfers between devices: 7.65 us -> 16.7 us
  Pallas kernels: 17.6 us -> 13.7 us
  local copies, waits for them, and re-layouts: 4.56 us -> 0.81 us
    ppermute x7 -> x3, starting transfers between devices: 16.3 us -> 4.82 us  [total_over(): lax.ppermute(values, axis, [(i, i ^ step) for i in range(size)])]
    ppermute x7 -> x3, waiting for transfers between devices: 0.02 us -> 4.67 us  [total_over(): lax.ppermute(values, axis, [(i, i ^ step) for i in range(size)])]
    unnamed x16 -> x2, local copies, waits for them, and re-layouts: 4.47 us -> 0.01 us
    ppermute x2, waiting for transfers between devices: 1.28 us -> 5.52 us  [the longest x1 4.09 us: regrid(): down_codes = lax.ppermute(high, 'band', up)]
    pallas_call x1, Pallas kernels: 6.31 us -> 2.97 us  [regrid(): pl.pallas_call(weigh_body, out_shape=(jax.ShapeDtypeStruct((columns, cell...]
    ppermute x1, waiting for transfers between devices: 1.94 us -> 4.15 us  [regrid(): from_down = lax.ppermute(to_up, 'band', up)]
    ppermute x2, starting transfers between devices: 5.84 us -> 3.66 us  [the longest x1 3.65 us: regrid(): up_codes = lax.ppermute(low, 'band', down)]
    ppermute x1, waiting for transfers between devices: 4.42 us -> 2.33 us  [regrid(): from_up = lax.ppermute(to_down, 'band', down)]
  transfers between devices with their start and end apart: 11 -> 7, of which waited for: 3 -> 6; matrix products, arithmetic and copies ran while one was open for 1% -> 3% of each run, Pallas kernels for 17% -> 2%
where the time goes in v2:
time: 45 us; the launch traced here: 44.7 us
  waiting for transfers between devices  16.7 us (37%)
  Pallas kernels  13.7 us (30%)
  starting transfers between devices  12.3 us (27%)
  local copies, waits for them, and re-layouts  0.81 us (2%)
  between operations  0.68 us (2%)
  other arithmetic  0.63 us (1%)
    pallas_call x1, Pallas kernels, regrid(): pl.pallas_call(local_body, out_shape=(jax.ShapeDtypeStruct((columns, tgt_...  6.28 us
    ppermute x3, starting transfers between devices, total_over(): lax.ppermute(values, axis, [(i, i ^ step) for i in range(size)])  4.82 us
    ppermute x3, waiting for transfers between devices, total_over(): lax.ppermute(values, axis, [(i, i ^ step) for i in range(size)])  4.67 us
    ppermute x1, waiting for transfers between devices, regrid(): from_down = lax.ppermute(to_up, 'band', up)  4.15 us
    ppermute x1, waiting for transfers between devices, regrid(): down_codes = lax.ppermute(high, 'band', up)  4.09 us
    ppermute x1, starting transfers between devices, regrid(): up_codes = lax.ppermute(low, 'band', down)  3.65 us
    pallas_call x1, Pallas kernels, regrid(): pl.pallas_call(weigh_body, out_shape=(jax.ShapeDtypeStruct((columns, cell...  2.97 us
    ppermute x1, waiting for transfers between devices, regrid(): from_up = lax.ppermute(to_down, 'band', down)  2.33 us
  transfers between devices with their start and end apart: 7, of which 6 were waited for; matrix products, arithmetic and copies ran while one was open for 3% of the time, Pallas kernels for 2%

profile of v2, /device:TPU:0, one launch (start us, length us, event | category | flops | bytes accessed | tf_op | source)
XLA Modules:
  0.0 44.7 jit_solution(15322114845041054831)
XLA Ops:
  0.6 3.0 %weigh.1 = (bf16[128,16384]{1,0:T(8,128)(2,1)S(1)}, f32[8,128]{1,0:T(8,128)S(1)}, bf16[17,128,128]{2,1,0:T(8,128)(2,1)S(1)}) custom-call(bf16[128,16384]{1,0:T(8,128)(2,1)} %bitcast.10, s32[1,16384]{1,0:T(1,128)} %bitcast.12, f32[1,16384]{1,0:T(1,128)} %bitcast.13, f32[1,4096]{1,0:T(1,128)} %bitcast.8, bf16[16,128,128]{2,1,0:T(8,128)(2,1)} %tiles_hbm.1), custom_call_target="tpu_custom_call" | custom-call | tf_op jit(solution)/shard_map/weigh/pallas_call | solution.py:255
  3.6 3.0 %collective-permute-start.2 = (f32[8,128]{1,0:T(8,128)S(1)}, f32[8,128]{1,0:T(8,128)S(1)}, u32[]{:S(2)}, u32[]{:S(2)}) collective-permute-start(f32[8,128]{1,0:T(8,128)S(1)} %get-tuple-element.20.totals), channel_id=1, source_target_pairs={{0,2},{2,0},{1,3},{3,1},{4,6},{6,4},{5,7},{7,5},{8,10},{10,8},{9,1... | collective-permute-start | bytes 12296 | tf_op jit(solution)/shard_map/ppermute | solution.py:215
  6.6 1.1 %edges.1 = (s32[32,32]{1,0:T(8,128)S(1)}, s32[32,32]{1,0:T(8,128)S(1)}, s32[32,32]{1,0:T(8,128)S(1)}) custom-call(s32[24,32]{1,0:T(8,128)} %bitcast.14, s32[24,32]{1,0:T(8,128)} %bitcast.15, s32[1,32]{1,0:T(1,128)} %bitcast.16), custom_call_target="tpu_custom_call" | custom-call | tf_op jit(solution)/shard_map/edges/pallas_call | solution.py:238
  7.7 3.7 %collective-permute-start = (s32[32,32]{1,0:T(8,128)S(1)}, s32[32,32]{1,0:T(8,128)S(1)}, u32[]{:S(2)}, u32[]{:S(2)}) collective-permute-start(s32[32,32]{1,0:T(8,128)S(1)} %get-tuple-element.17), channel_id=1, source_target_pairs={{4,0},{8,4},{12,8},{0,12},{5,1},{9,5},{13,9},{1,13},{6,2},{10,6},{... | collective-permute-start | bytes 12296 | tf_op jit(solution)/shard_map/ppermute | solution.py:252
  11.4 0.0 collective-permute-start.1
  11.4 0.0 collective-permute-done.2
  11.4 1.4 %collective-permute-done.up_codes = s32[32,32]{1,0:T(8,128)S(1)} collective-permute-done((s32[32,32]{1,0:T(8,128)S(1)}, s32[32,32]{1,0:T(8,128)S(1)}, u32[]{:S(2)}, u32[]{:S(2)}) %collective-permute-start) | collective-permute-done | bytes 4128 | tf_op jit(solution)/shard_map/ppermute | solution.py:252
  12.8 4.1 %collective-permute-done.1.down_codes = s32[32,32]{1,0:T(8,128)S(1)} collective-permute-done((s32[32,32]{1,0:T(8,128)S(1)}, s32[32,32]{1,0:T(8,128)S(1)}, u32[]{:S(2)}, u32[]{:S(2)}) %collective-permute-start.1) | collective-permute-done | bytes 4128 | tf_op jit(solution)/shard_map/ppermute | solution.py:253
  16.9 0.0 copy-start
  16.9 1.8 %reach.1 = (bf16[128,1024]{1,0:T(8,128)(2,1)S(1)}, bf16[128,1024]{1,0:T(8,128)(2,1)S(1)}, f32[8,128]{1,0:T(8,128)S(1)}) custom-call(s32[32,32]{1,0:T(8,128)S(1)} %collective-permute-done.up_codes, s32[32,32]{1,0:T(8,128)S(1)} %collective-permute-done.1.down_codes, bf16[128,16384]{1,0:T(8,128)(2,1)S(1)} %get-tuple-element.15.weighted, ...), custom_call_target="tpu_custom_call" | custom-call | tf_op jit(solution)/shard_map/reach/pallas_call | solution.py:282
  18.7 6.3 %local.1 = (f32[128,4096]{1,0:T(8,128)S(1)}, f32[8,128]{1,0:T(8,128)S(1)}) custom-call(s32[32,32]{1,0:T(8,128)S(1)} %get-tuple-element.14.codes, bf16[128,16384]{1,0:T(8,128)(2,1)S(1)} %get-tuple-element.15.weighted, bf16[17,128,128]{2,1,0:T(8,128)(2,1)S(1)} %get-tuple-element.16.tiles, f32[8,128]{1,0:T(8,128)S(1)} %get-tuple-element.19.reach_sums, ...), custom_call_target="tpu_custom_call" | custom-call | tf_op jit(solution)/shard_map/local/pallas_call | solution.py:299
  25.0 0.1 collective-permute-start.5
  25.1 3.6 %collective-permute-done.5 = f32[8,128]{1,0:T(8,128)S(1)} collective-permute-done((f32[8,128]{1,0:T(8,128)S(1)}, f32[8,128]{1,0:T(8,128)S(1)}, u32[]{:S(2)}, u32[]{:S(2)}) %collective-permute-start.5) | collective-permute-done | bytes 4128 | tf_op jit(solution)/shard_map/ppermute | solution.py:215
  28.7 1.7 %collective-permute-start.6 = (f32[8,128]{1,0:T(8,128)S(1)}, f32[8,128]{1,0:T(8,128)S(1)}, u32[]{:S(2)}, u32[]{:S(2)}) collective-permute-start(f32[8,128]{1,0:T(8,128)S(1)} %add.10), channel_id=1, source_target_pairs={{0,8},{4,12},{8,0},{12,4},{1,9},{5,13},{9,1},{13,5},{2,10},{6,14},... | collective-permute-start | bytes 12296 | tf_op jit(solution)/shard_map/ppermute | solution.py:215
  30.4 2.0 %collective-permute-start.3 = (bf16[128,1024]{1,0:T(8,128)(2,1)S(1)}, bf16[128,1024]{1,0:T(8,128)(2,1)S(1)}, u32[]{:S(2)}, u32[]{:S(2)}) collective-permute-start(bf16[128,1024]{1,0:T(8,128)(2,1)S(1)} %get-tuple-element.22), channel_id=1, source_target_pairs={{0,4},{4,8},{8,12},{12,0},{1,5},{5,9},{9,13},{13,1},{2,6},{6,10},{... | collective-permute-start | bytes 786440 | tf_op jit(solution)/shard_map/ppermute | solution.py:296
  32.4 1.8 %collective-permute-start.4 = (bf16[128,1024]{1,0:T(8,128)(2,1)S(1)}, bf16[128,1024]{1,0:T(8,128)(2,1)S(1)}, u32[]{:S(2)}, u32[]{:S(2)}) collective-permute-start(bf16[128,1024]{1,0:T(8,128)(2,1)S(1)} %get-tuple-element.23), channel_id=1, source_target_pairs={{4,0},{8,4},{12,8},{0,12},{5,1},{9,5},{13,9},{1,13},{6,2},{10,6},{... | collective-permute-start | bytes 786440 | tf_op jit(solution)/shard_map/ppermute | solution.py:297
  34.2 1.1 %collective-permute-done.6 = f32[8,128]{1,0:T(8,128)S(1)} collective-permute-done((f32[8,128]{1,0:T(8,128)S(1)}, f32[8,128]{1,0:T(8,128)S(1)}, u32[]{:S(2)}, u32[]{:S(2)}) %collective-permute-start.6) | collective-permute-done | bytes 4128 | tf_op jit(solution)/shard_map/ppermute | solution.py:215
  35.3 0.1 div.27
  35.4 0.7 %div.25 = f32[4,4,8]{2,1,0:T(4,128)} reshape(f32[128]{0:T(128)S(1)} %get-tuple-element.26) | data formatting | bytes 1024 | tf_op jit(solution)/shard_map/div | solution.py:327
  36.2 0.6 %broadcast_multiply_fusion = f32[4,8]{1,0:T(4,128)} fusion(f32[4,8]{1,0:T(4,128)S(1)} %reduce_sum.9), kind=kLoop, calls=%fused_computation | loop fusion | flops 32 | bytes 256 | tf_op jit(solution)/shard_map/div | solution.py:328
  36.7 4.1 %collective-permute-done.3.from_down = bf16[128,1024]{1,0:T(8,128)(2,1)S(1)} collective-permute-done((bf16[128,1024]{1,0:T(8,128)(2,1)S(1)}, bf16[128,1024]{1,0:T(8,128)(2,1)S(1)}, u32[]{:S(2)}, u32[]{:S(2)}) %collective-permute-start.3) | collective-permute-done | bytes 262176 | tf_op jit(solution)/shard_map/ppermute | solution.py:296
  40.9 2.3 %collective-permute-done.4.from_up = bf16[128,1024]{1,0:T(8,128)(2,1)S(1)} collective-permute-done((bf16[128,1024]{1,0:T(8,128)(2,1)S(1)}, bf16[128,1024]{1,0:T(8,128)(2,1)S(1)}, u32[]{:S(2)}, u32[]{:S(2)}) %collective-permute-start.4) | collective-permute-done | bytes 262176 | tf_op jit(solution)/shard_map/ppermute | solution.py:297
  43.2 0.0 copy-done
  43.2 1.5 %finish.1 = f32[128,4096]{1,0:T(8,128)} custom-call(f32[128,4096]{1,0:T(8,128)S(1)} %get-tuple-element.21.raw, bf16[128,1024]{1,0:T(8,128)(2,1)S(1)} %collective-permute-done.3.from_down, bf16[128,1024]{1,0:T(8,128)(2,1)S(1)} %collective-permute-done.4.from_up, f32[1,4096]{1,0:T(1,128)S(1)} %bitcast.9, f32[8,128]{1,0:T(8,128)S(1)} %add.11.totals), custom_call_target="tpu_custom_call" | custom-call | tf_op jit(solution)/shard_map/finish/pallas_call | solution.py:314
  (5 shorter events, 0.0 us)
Async XLA Ops:
  3.6 7.8 %collective-permute-start.2 = (f32[8,128]{1,0:T(8,128)S(1)}, f32[8,128]{1,0:T(8,128)S(1)}, u32[]{:S(2)}, u32[]{:S(2)}) collective-permute-start(f32[8,128]{1,0:T(8,128)S(1)} %get-tuple-element.20.totals), channel_id=1, source_target_pairs={{0,2},{2,0},{1,3},{3,1},{4,6},{6,4},{5,7},{7,5},{8,10},{10,8},{9,1... | collective-permute-start | bytes 12296 | tf_op jit(solution)/shard_map/ppermute | solution.py:215
  7.7 5.1 %collective-permute-start = (s32[32,32]{1,0:T(8,128)S(1)}, s32[32,32]{1,0:T(8,128)S(1)}, u32[]{:S(2)}, u32[]{:S(2)}) collective-permute-start(s32[32,32]{1,0:T(8,128)S(1)} %get-tuple-element.17), channel_id=1, source_target_pairs={{4,0},{8,4},{12,8},{0,12},{5,1},{9,5},{13,9},{1,13},{6,2},{10,6},{... | collective-permute-start | bytes 12296 | tf_op jit(solution)/shard_map/ppermute | solution.py:252
  11.4 5.5 %collective-permute-start.1 = (s32[32,32]{1,0:T(8,128)S(1)}, s32[32,32]{1,0:T(8,128)S(1)}, u32[]{:S(2)}, u32[]{:S(2)}) collective-permute-start(s32[32,32]{1,0:T(8,128)S(1)} %get-tuple-element.18), channel_id=1, source_target_pairs={{0,4},{4,8},{8,12},{12,0},{1,5},{5,9},{9,13},{13,1},{2,6},{6,10},{... | collective-permute-start | bytes 12296 | tf_op jit(solution)/shard_map/ppermute | solution.py:253
  16.9 26.3 %copy-start = (f32[4096]{0:T(1024)S(1)}, f32[4096]{0:T(1024)}, u32[]{:S(2)}) copy-start(f32[4096]{0:T(1024)} %param.11) | copy-start | bytes 49156
  25.0 3.7 %collective-permute-start.5 = (f32[8,128]{1,0:T(8,128)S(1)}, f32[8,128]{1,0:T(8,128)S(1)}, u32[]{:S(2)}, u32[]{:S(2)}) collective-permute-start(f32[8,128]{1,0:T(8,128)S(1)} %get-tuple-element.24), channel_id=1, source_target_pairs={{0,4},{4,0},{8,12},{12,8},{1,5},{5,1},{9,13},{13,9},{2,6},{6,2},{1... | collective-permute-start | bytes 12296 | tf_op jit(solution)/shard_map/ppermute | solution.py:215
  28.7 6.6 %collective-permute-start.6 = (f32[8,128]{1,0:T(8,128)S(1)}, f32[8,128]{1,0:T(8,128)S(1)}, u32[]{:S(2)}, u32[]{:S(2)}) collective-permute-start(f32[8,128]{1,0:T(8,128)S(1)} %add.10), channel_id=1, source_target_pairs={{0,8},{4,12},{8,0},{12,4},{1,9},{5,13},{9,1},{13,5},{2,10},{6,14},... | collective-permute-start | bytes 12296 | tf_op jit(solution)/shard_map/ppermute | solution.py:215
  30.4 10.5 %collective-permute-start.3 = (bf16[128,1024]{1,0:T(8,128)(2,1)S(1)}, bf16[128,1024]{1,0:T(8,128)(2,1)S(1)}, u32[]{:S(2)}, u32[]{:S(2)}) collective-permute-start(bf16[128,1024]{1,0:T(8,128)(2,1)S(1)} %get-tuple-element.22), channel_id=1, source_target_pairs={{0,4},{4,8},{8,12},{12,0},{1,5},{5,9},{9,13},{13,1},{2,6},{6,10},{... | collective-permute-start | bytes 786440 | tf_op jit(solution)/shard_map/ppermute | solution.py:296
  32.4 10.8 %collective-permute-start.4 = (bf16[128,1024]{1,0:T(8,128)(2,1)S(1)}, bf16[128,1024]{1,0:T(8,128)(2,1)S(1)}, u32[]{:S(2)}, u32[]{:S(2)}) collective-permute-start(bf16[128,1024]{1,0:T(8,128)(2,1)S(1)} %get-tuple-element.23), channel_id=1, source_target_pairs={{4,0},{8,4},{12,8},{0,12},{5,1},{9,5},{13,9},{1,13},{6,2},{10,6},{... | collective-permute-start | bytes 786440 | tf_op jit(solution)/shard_map/ppermute | solution.py:297

commit v3 on v2

--- a/solution.py
+++ b/solution.py
@@ -12,8 +12,8 @@
 HALO_BLK = 32
 CHUNK = 4
 CHUNK_BITS = 2
-UNROLL = 4
-UNROLL_BITS = 2
+UNROLL = 8
+UNROLL_BITS = 3
 PIECES = 8
 PLACE_BITS = 16
 
@@ -69,9 +69,29 @@
     own[...] = packed(alive & (block >= 0) & (block < own_blocks), code, blank)
 
 
+def cell_weights(codes, tiles, tile_count, own_blocks):
+    slots, targets = codes.shape[0] - 8, codes.shape[1]
+    tile = tiles.shape[1]
+    last = (((1,), (1,)), ((), ()))
+    line = jnp.concatenate([codes[k : k + 1, :] for k in range(slots)], axis=1)
+    length = slots * targets
+    blocks = lax.broadcasted_iota(jnp.int32, (own_blocks, length), 0)
+    kinds = lax.broadcasted_iota(jnp.int32, (tile_count, length), 0)
+    reads = jnp.where(blocks == (line & ((1 << PLACE_BITS) - 1)), 1.0, 0.0).astype(jnp.bfloat16)
+    uses = jnp.where(kinds == (line >> PLACE_BITS), 1.0, 0.0).astype(jnp.bfloat16)
+    counts = lax.dot_general(reads, uses, last, preferred_element_type=jnp.float32)
+    flat = tiles[pl.ds(0, tile_count)].reshape(tile_count * tile, tiles.shape[2])
+    ones = jnp.ones((8, tiles.shape[2]), jnp.bfloat16)
+    sums = lax.dot_general(ones, flat, last, preferred_element_type=jnp.float32)
+    sums = jnp.concatenate([sums[0:1, k * tile : (k + 1) * tile] for k in range(tile_count)], axis=0)
+    return jnp.dot(
+        counts, sums, precision=lax.Precision.HIGHEST, preferred_element_type=jnp.float32
+    )
+
+
 def weigh_body(
-    fields_hbm, mask_hbm, area_hbm, target_hbm, tiles_hbm,
-    weighted, totals, tiles, fields, mask, source, target, sems,
+    fields_hbm, mask_hbm, area_hbm, target_hbm, tiles_hbm, codes,
+    weighted, totals, tiles, fields, mask, source, target, spread, sems,
 ):
     columns, cells = weighted.shape
     tile_count, tile, lanes = tiles_hbm.shape
@@ -91,34 +111,39 @@
         )
         for n in range(PIECES)
     ]
-    for copy in small[:3] + copies + small[3:]:
+    for copy in small + copies:
         copy.start()
     tiles[tile_count] = jnp.zeros((tile, lanes), tiles.dtype)
-    for copy in small[:3]:
+    for copy in small:
         copy.wait()
+    spread[...] = cell_weights(codes, tiles, tile_count, cells // tile)
     area = jnp.sum(target[...], axis=1, keepdims=True)
-    acc = jnp.zeros((columns, tile), jnp.float32)
+    accs = (jnp.zeros((columns, tile), jnp.float32),) * 2
     for n in range(PIECES):
         copies[n].wait()
 
-        def one(k, acc):
+        def one(k, accs):
+            acc, reached = accs
             at = pl.ds(pl.multiple_of(n * piece + k * step, step), step)
             factor = source[:, at] * mask[:, at].astype(jnp.float32)
             value = (factor * fields[:, at].astype(jnp.float32)).astype(jnp.bfloat16)
             weighted[:, at] = value
             wide = value.astype(jnp.float32)
             for q in range(4):
-                acc = acc + wide[:, q * tile : (q + 1) * tile]
-            return acc
-
-        acc = lax.fori_loop(0, piece // step, one, acc)
-    own = row_of(acc)
+                part = wide[:, q * tile : (q + 1) * tile]
+                acc = acc + part
+                reached = reached + part * spread[pl.ds(n * (piece // tile) + k * 4 + q, 1), :]
+            return acc, reached
+
+        accs = lax.fori_loop(0, piece // step, one, accs)
+    own = row_of(accs[0])
+    reached = row_of(accs[1])
     rows = lax.broadcasted_iota(jnp.int32, (8, columns), 0)
-    totals[...] = jnp.where(rows == 0, own, jnp.where(rows == 1, area, 0.0))
-    small[3].wait()
-
-
-def run_items(codes, first, weighted, tiles, out, work):
+    rest = jnp.where(rows == 1, area, jnp.where(rows == 2, reached, 0.0))
+    totals[...] = jnp.where(rows == 0, own, rest)
+
+
+def run_items(codes, weighted, tiles, out, work):
     tile = tiles.shape[1]
     slots = codes.shape[0] - 8
     chunks = slots // CHUNK
@@ -127,7 +152,7 @@
     def one_target(n, items):
         for q in range(chunks):
             work[items + q] = (q << PLACE_BITS) + n
-        return items + ((codes[slots, first + n] + CHUNK - 1) >> CHUNK_BITS)
+        return items + ((codes[slots, n] + CHUNK - 1) >> CHUNK_BITS)
 
     count = lax.fori_loop(0, out.shape[1] // tile, one_target, 0)
     for q in range(UNROLL):
@@ -138,7 +163,7 @@
         for u in range(UNROLL):
             item = work[step * UNROLL + u]
             row = (item >> PLACE_BITS) * CHUNK
-            column = first + (item & ((1 << PLACE_BITS) - 1))
+            column = item & ((1 << PLACE_BITS) - 1)
             left, right = [], []
             for q in range(CHUNK):
                 code = codes[row + q, column]
@@ -159,30 +184,28 @@
         return nothing
 
     lax.fori_loop(0, (count + UNROLL - 1) >> UNROLL_BITS, one, 0)
+
+
+def reach_body(codes, weighted, tiles, totals, to_up, to_down, sums, out, work):
+    tile = tiles.shape[1]
+    run_items(codes, weighted, tiles, out, work)
+    half = to_up.shape[1]
+    to_up[...] = out[:, :half].astype(to_up.dtype)
+    to_down[...] = out[:, half:].astype(to_down.dtype)
     acc = out[:, :tile]
     for n in range(1, out.shape[1] // tile):
         acc = acc + out[:, n * tile : (n + 1) * tile]
-    return acc
-
-
-def reach_body(up_codes, down_codes, weighted, tiles, to_up, to_down, sums, first, second, work):
-    tile = tiles.shape[1]
-    acc = run_items(up_codes, 0, weighted, tiles, first, work)
-    start = down_codes.shape[1] - second.shape[1] // tile
-    to_up[...] = first[...].astype(to_up.dtype)
-    acc = acc + run_items(down_codes, start, weighted, tiles, second, work)
-    to_down[...] = second[...].astype(to_down.dtype)
-    sums[...] = jnp.broadcast_to(row_of(acc), sums.shape)
-
-
-def local_body(codes, weighted, tiles, reach_sums, totals, peers, raw, sums, work):
-    acc = run_items(codes, 0, weighted, tiles, raw, work)
-    reached = reach_sums[0:1] + row_of(acc)
     rows = lax.broadcasted_iota(jnp.int32, sums.shape, 0)
-    sums[...] = jnp.where(rows == 2, reached, jnp.where(rows == 3, peers[0:1], totals[...]))
-
-
-def finish_body(raw, from_down, from_up, target, totals, out_hbm, staged, sems):
+    sums[...] = totals[...] + jnp.where(rows == 2, row_of(acc), 0.0)
+
+
+def local_body(codes, weighted, tiles, raw, work):
+    run_items(codes, weighted, tiles, raw, work)
+
+
+def finish_body(
+    raw, from_down, from_up, target, totals, out_hbm, conserved, ensemble, staged, sems
+):
     columns, cells = raw.shape
     edge = from_down.shape[1]
     piece = edge // 2
@@ -202,6 +225,16 @@
         staged[:, at] = value / target[:, at] + spread
         copies.append(pltpu.make_async_copy(staged.at[:, at], out_hbm.at[:, at], sems.at[n]))
         copies[n].start()
+    members, fields, snapshots = conserved.shape
+    own = totals[0:1] / totals[1:2]
+    every = totals[3:4] / totals[1:2]
+    for f in range(fields):
+        mean = jnp.zeros((1, snapshots), jnp.float32)
+        for m in range(members):
+            begin = (m * fields + f) * snapshots
+            conserved[m, f : f + 1, :] = own[:, begin : begin + snapshots]
+            mean = mean + every[:, begin : begin + snapshots]
+        ensemble[f : f + 1, :] = mean / MEMBERS
     for copy in copies:
         copy.wait()
 
@@ -210,6 +243,11 @@
     size = lax.axis_size(axis)
     if size & (size - 1):
         return lax.psum(values, axis)
+    if size == 4:
+        terms = [values]
+        for step in range(1, size):
+            terms.append(lax.ppermute(values, axis, [(i, i ^ step) for i in range(size)]))
+        return (terms[0] + terms[1]) + (terms[2] + terms[3])
     step = 1
     while step < size:
         values = values + lax.ppermute(values, axis, [(i, i ^ step) for i in range(size)])
@@ -259,13 +297,14 @@
             jax.ShapeDtypeStruct((8, columns), f32),
             jax.ShapeDtypeStruct((tile_count + 1, tile, tile), jnp.bfloat16),
         ),
-        in_specs=[ANY] * 5,
+        in_specs=[ANY] * 5 + [VMEM],
         out_specs=(VMEM,) * 3,
         scratch_shapes=[
             pltpu.VMEM((columns, cells), jnp.bfloat16),
             pltpu.VMEM((1, cells), jnp.int32),
             pltpu.VMEM((1, cells), f32),
             pltpu.VMEM((1, tgt_count * tile), f32),
+            pltpu.VMEM((own_blocks, tile), f32),
             pltpu.SemaphoreType.DMA((PIECES + 4,)),
         ],
         compiler_params=params(16),
@@ -276,46 +315,52 @@
         in_hbm(source_area.reshape(1, cells)),
         in_hbm(target_area.reshape(1, tgt_count * tile)),
         in_hbm(weight_tiles),
+        codes,
     )
     peers = total_over(totals, "mem")
 
-    to_up, to_down, reach_sums = pl.pallas_call(
+    reach_codes = jnp.concatenate([up_codes[:, :edge], down_codes[:, tgt_count - edge :]], axis=1)
+    to_up, to_down, sums = pl.pallas_call(
         reach_body,
         out_shape=(
             jax.ShapeDtypeStruct((columns, edge * tile), jnp.bfloat16),
             jax.ShapeDtypeStruct((columns, edge * tile), jnp.bfloat16),
             jax.ShapeDtypeStruct((8, columns), f32),
         ),
-        in_specs=[SMEM, SMEM, VMEM, VMEM],
-        out_specs=(VMEM, VMEM, VMEM),
-        scratch_shapes=[pltpu.VMEM((columns, edge * tile), f32)] * 2
-        + [pltpu.SMEM((edge * work_size + 8,), jnp.int32)],
+        in_specs=[SMEM, VMEM, VMEM, VMEM],
+        out_specs=(VMEM,) * 3,
+        scratch_shapes=[
+            pltpu.VMEM((columns, 2 * edge * tile), f32),
+            pltpu.SMEM((2 * edge * work_size + 16,), jnp.int32),
+        ],
         compiler_params=params(8),
         name="reach",
-    )(up_codes, down_codes, weighted, tiles)
+    )(reach_codes, weighted, tiles, totals)
     from_down = lax.ppermute(to_up, "band", up)
     from_up = lax.ppermute(to_down, "band", down)
-
-    raw, sums = pl.pallas_call(
+    rows = lax.broadcasted_iota(jnp.int32, sums.shape, 0)
+    totals = total_over(jnp.where(rows == 3, peers[0:1], sums), "band")
+
+    raw = pl.pallas_call(
         local_body,
+        out_shape=jax.ShapeDtypeStruct((columns, tgt_count * tile), f32),
+        in_specs=[SMEM, VMEM, VMEM],
+        out_specs=VMEM,
+        scratch_shapes=[pltpu.SMEM((tgt_count * work_size + 16,), jnp.int32)],
+        compiler_params=params(8),
+        name="local",
+    )(codes, weighted, tiles)
+
+    piece_count = 2 * tgt_count // edge
+    regridded, conserved, ensemble = pl.pallas_call(
+        finish_body,
         out_shape=(
             jax.ShapeDtypeStruct((columns, tgt_count * tile), f32),
-            jax.ShapeDtypeStruct((8, columns), f32),
+            jax.ShapeDtypeStruct((members, fields, snapshots), f32),
+            jax.ShapeDtypeStruct((fields, snapshots), f32),
         ),
-        in_specs=[SMEM, VMEM, VMEM, VMEM, VMEM, VMEM],
-        out_specs=(VMEM, VMEM),
-        scratch_shapes=[pltpu.SMEM((tgt_count * work_size + 8,), jnp.int32)],
-        compiler_params=params(8),
-        name="local",
-    )(codes, weighted, tiles, reach_sums, totals, peers)
-    totals = total_over(sums, "band")
-
-    piece_count = 2 * tgt_count // edge
-    regridded = pl.pallas_call(
-        finish_body,
-        out_shape=jax.ShapeDtypeStruct((columns, tgt_count * tile), f32),
         in_specs=[VMEM] * 5,
-        out_specs=ANY,
+        out_specs=(ANY, VMEM, VMEM),
         scratch_shapes=[
             pltpu.VMEM((columns, tgt_count * tile), f32),
             pltpu.SemaphoreType.DMA((piece_count,)),
@@ -324,8 +369,6 @@
         name="finish",
     )(raw, from_down, from_up, target_area.reshape(1, tgt_count * tile), totals)
 
-    conserved = (totals[0] / totals[1]).reshape(members, fields, snapshots)
-    ensemble = jnp.sum((totals[3] / totals[1]).reshape(members, fields, snapshots), axis=0) / MEMBERS
     return regridded.reshape(members, fields, snapshots, tgt_count * tile), conserved, ensemble
 
 

time: 45 us -> 33.7 us (0.75)
  waiting for transfers between devices: 16.7 us -> 2.58 us
  starting transfers between devices: 12.3 us -> 15.2 us
  Pallas kernels: 13.7 us -> 14.7 us
  local copies, waits for them, and re-layouts: 0.81 us -> 0.08 us
    ppermute x1, waiting for transfers between devices: 4.15 us -> 0.01 us  [regrid(): from_down = lax.ppermute(to_up, 'band', up)]
    ppermute x1, waiting for transfers between devices: 4.09 us -> 0.01 us  [regrid(): down_codes = lax.ppermute(high, 'band', up)]
    ppermute x1, starting transfers between devices: 0.01 us -> 3.1 us  [regrid(): down_codes = lax.ppermute(high, 'band', up)]
    ppermute x1, waiting for transfers between devices: 2.33 us -> 0.01 us  [regrid(): from_up = lax.ppermute(to_down, 'band', down)]
    ppermute x3 -> x4, waiting for transfers between devices: 4.67 us -> 2.57 us  [total_over(): lax.ppermute(values, axis, [(i, i ^ step) for i in range(size)])]
    ppermute x1, starting transfers between devices: 1.8 us -> 3.39 us  [regrid(): from_up = lax.ppermute(to_down, 'band', down)]
    ppermute x1, starting transfers between devices: 3.65 us -> 2.09 us  [regrid(): up_codes = lax.ppermute(low, 'band', down)]
    ppermute x1, starting transfers between devices: 2.02 us -> 0.49 us  [regrid(): from_down = lax.ppermute(to_up, 'band', up)]
  transfers between devices with their start and end apart: 7 -> 8, of which waited for: 6 -> 2; matrix products, arithmetic and copies ran while one was open for 3% -> 1% of each run, Pallas kernels for 2% -> 29%
where the time goes in v3:
time: 33.7 us; the launch traced here: 33.5 us
  starting transfers between devices  15.2 us (45%)
  Pallas kernels  14.7 us (44%)
  waiting for transfers between devices  2.58 us (8%)
  between operations  0.7 us (2%)
    ppermute x4, starting transfers between devices, total_over(): lax.ppermute(values, axis, [(i, i ^ step) for i in range(size)])  6.1 us
    pallas_call x1, Pallas kernels, regrid(): pl.pallas_call(local_body, out_shape=jax.ShapeDtypeStruct((columns, tgt_c...  5.42 us
    pallas_call x1, Pallas kernels, regrid(): pl.pallas_call(weigh_body, out_shape=(jax.ShapeDtypeStruct((columns, cell...  4.22 us
    ppermute x1, starting transfers between devices, regrid(): from_up = lax.ppermute(to_down, 'band', down)  3.39 us
    ppermute x1, starting transfers between devices, regrid(): down_codes = lax.ppermute(high, 'band', up)  3.1 us
    ppermute x4, waiting for transfers between devices, total_over(): lax.ppermute(values, axis, [(i, i ^ step) for i in range(size)])  2.57 us
    pallas_call x1, Pallas kernels, regrid(): pl.pallas_call(finish_body, out_shape=(jax.ShapeDtypeStruct((columns, tgt...  2.28 us
    ppermute x1, starting transfers between devices, regrid(): up_codes = lax.ppermute(low, 'band', down)  2.09 us
  transfers between devices with their start and end apart: 8, of which 2 were waited for; matrix products, arithmetic and copies ran while one was open for 1% of the time, Pallas kernels for 29%

profile of v3, /device:TPU:0, one launch (start us, length us, event | category | flops | bytes accessed | tf_op | source)
XLA Modules:
  0.0 33.5 jit_solution(12654268609285130074)
XLA Ops:
  0.6 1.1 %edges.1 = (s32[32,32]{1,0:T(8,128)S(1)}, s32[32,32]{1,0:T(8,128)S(1)}, s32[32,32]{1,0:T(8,128)S(1)}) custom-call(s32[24,32]{1,0:T(8,128)} %bitcast.17, s32[24,32]{1,0:T(8,128)} %bitcast.18, s32[1,32]{1,0:T(1,128)} %bitcast.19), custom_call_target="tpu_custom_call" | custom-call | tf_op jit(solution)/shard_map/edges/pallas_call | solution.py:276
  1.7 3.1 %collective-permute-start.1 = (s32[32,32]{1,0:T(8,128)S(1)}, s32[32,32]{1,0:T(8,128)S(1)}, u32[]{:S(2)}, u32[]{:S(2)}) collective-permute-start(s32[32,32]{1,0:T(8,128)S(1)} %get-tuple-element.19), channel_id=1, source_target_pairs={{0,4},{4,8},{8,12},{12,0},{1,5},{5,9},{9,13},{13,1},{2,6},{6,10},{... | collective-permute-start | bytes 12296 | tf_op jit(solution)/shard_map/ppermute | solution.py:291
  4.8 2.1 %collective-permute-start = (s32[32,32]{1,0:T(8,128)S(1)}, s32[32,32]{1,0:T(8,128)S(1)}, u32[]{:S(2)}, u32[]{:S(2)}) collective-permute-start(s32[32,32]{1,0:T(8,128)S(1)} %get-tuple-element.18), channel_id=1, source_target_pairs={{4,0},{8,4},{12,8},{0,12},{5,1},{9,5},{13,9},{1,13},{6,2},{10,6},{... | collective-permute-start | bytes 12296 | tf_op jit(solution)/shard_map/ppermute | solution.py:290
  6.9 4.2 %weigh.1 = (bf16[128,16384]{1,0:T(8,128)(2,1)S(1)}, f32[8,128]{1,0:T(8,128)S(1)}, bf16[17,128,128]{2,1,0:T(8,128)(2,1)S(1)}) custom-call(bf16[128,16384]{1,0:T(8,128)(2,1)} %bitcast.13, s32[1,16384]{1,0:T(1,128)} %bitcast.14, f32[1,16384]{1,0:T(1,128)} %bitcast.15, f32[1,4096]{1,0:T(1,128)} %bitcast.11, bf16[16,128,128]{2,1,0:T(8,128)(2,1)} %tiles_hbm.1, ...), custom_call_target="tpu_custom_call" | custom-call | tf_op jit(solution)/shard_map/weigh/pallas_call | solution.py:293
  11.1 1.7 %collective-permute-start.4 = (f32[8,128]{1,0:T(8,128)S(1)}, f32[8,128]{1,0:T(8,128)S(1)}, u32[]{:S(2)}, u32[]{:S(2)}) collective-permute-start(f32[8,128]{1,0:T(8,128)S(1)} %get-tuple-element.20.totals), channel_id=1, source_target_pairs={{0,2},{2,0},{1,3},{3,1},{4,6},{6,4},{5,7},{7,5},{8,10},{10,8},{9,1... | collective-permute-start | bytes 12296 | tf_op jit(solution)/shard_map/ppermute | solution.py:253
  12.8 2.0 %collective-permute-done.4 = f32[8,128]{1,0:T(8,128)S(1)} collective-permute-done((f32[8,128]{1,0:T(8,128)S(1)}, f32[8,128]{1,0:T(8,128)S(1)}, u32[]{:S(2)}, u32[]{:S(2)}) %collective-permute-start.4) | collective-permute-done | bytes 4128 | tf_op jit(solution)/shard_map/ppermute | solution.py:253
  14.8 0.0 collective-permute-done.1
  14.8 0.1 slice.13
  14.9 0.0 collective-permute-done
  14.9 0.1 pad_add_fusion.codes
  15.0 1.8 %reach.1 = (bf16[128,1024]{1,0:T(8,128)(2,1)S(1)}, bf16[128,1024]{1,0:T(8,128)(2,1)S(1)}, f32[8,128]{1,0:T(8,128)S(1)}) custom-call(s32[32,16]{1,0:T(8,128)S(1)} %pad_add_fusion.codes, bf16[128,16384]{1,0:T(8,128)(2,1)S(1)} %get-tuple-element.16.weighted, bf16[17,128,128]{2,1,0:T(8,128)(2,1)S(1)} %get-tuple-element.17.tiles, ...), custom_call_target="tpu_custom_call" | custom-call | tf_op jit(solution)/shard_map/reach/pallas_call | solution.py:323
  16.7 0.0 copy-start
  16.7 0.5 %collective-permute-start.2 = (bf16[128,1024]{1,0:T(8,128)(2,1)S(1)}, bf16[128,1024]{1,0:T(8,128)(2,1)S(1)}, u32[]{:S(2)}, u32[]{:S(2)}) collective-permute-start(bf16[128,1024]{1,0:T(8,128)(2,1)S(1)} %get-tuple-element.21), channel_id=1, source_target_pairs={{0,4},{4,8},{8,12},{12,0},{1,5},{5,9},{9,13},{13,1},{2,6},{6,10},{... | collective-permute-start | bytes 786440 | tf_op jit(solution)/shard_map/ppermute | solution.py:339
  17.2 3.4 %collective-permute-start.3 = (bf16[128,1024]{1,0:T(8,128)(2,1)S(1)}, bf16[128,1024]{1,0:T(8,128)(2,1)S(1)}, u32[]{:S(2)}, u32[]{:S(2)}) collective-permute-start(bf16[128,1024]{1,0:T(8,128)(2,1)S(1)} %get-tuple-element.22), channel_id=1, source_target_pairs={{4,0},{8,4},{12,8},{0,12},{5,1},{9,5},{13,9},{1,13},{6,2},{10,6},{... | collective-permute-start | bytes 786440 | tf_op jit(solution)/shard_map/ppermute | solution.py:340
  20.6 0.1 broadcast_select_fusion
  20.7 0.0 collective-permute-start.5
  20.7 0.7 %collective-permute-start.6 = (f32[8,128]{1,0:T(8,128)S(1)}, f32[8,128]{1,0:T(8,128)S(1)}, u32[]{:S(2)}, u32[]{:S(2)}) collective-permute-start(f32[8,128]{1,0:T(8,128)S(1)} %broadcast_select_fusion), channel_id=1, source_target_pairs={{0,8},{4,12},{8,0},{12,4},{1,9},{5,13},{9,1},{13,5},{2,10},{6,14},... | collective-permute-start | bytes 12296 | tf_op jit(solution)/shard_map/ppermute | solution.py:249
  21.4 3.7 %collective-permute-start.7 = (f32[8,128]{1,0:T(8,128)S(1)}, f32[8,128]{1,0:T(8,128)S(1)}, u32[]{:S(2)}, u32[]{:S(2)}) collective-permute-start(f32[8,128]{1,0:T(8,128)S(1)} %broadcast_select_fusion), channel_id=1, source_target_pairs={{0,12},{4,8},{8,4},{12,0},{1,13},{5,9},{9,5},{13,1},{2,14},{6,10},... | collective-permute-start | bytes 12296 | tf_op jit(solution)/shard_map/ppermute | solution.py:249
  25.1 5.4 %local.1.raw = f32[128,4096]{1,0:T(8,128)S(1)} custom-call(s32[32,32]{1,0:T(8,128)S(1)} %get-tuple-element.15.codes, bf16[128,16384]{1,0:T(8,128)(2,1)S(1)} %get-tuple-element.16.weighted, bf16[17,128,128]{2,1,0:T(8,128)(2,1)S(1)} %get-tuple-element.17.tiles), custom_call_target="tpu_custom_call" | custom-call | tf_op jit(solution)/shard_map/local/pallas_call | solution.py:344
  30.5 0.0 collective-permute-done.5
  30.5 0.0 collective-permute-done.6
  30.5 0.6 %collective-permute-done.7 = f32[8,128]{1,0:T(8,128)S(1)} collective-permute-done((f32[8,128]{1,0:T(8,128)S(1)}, f32[8,128]{1,0:T(8,128)S(1)}, u32[]{:S(2)}, u32[]{:S(2)}) %collective-permute-start.7) | collective-permute-done | bytes 4128 | tf_op jit(solution)/shard_map/ppermute | solution.py:249
  31.1 0.1 add_add_fusion.totals
  31.2 0.0 collective-permute-done.2.from_down
  31.2 0.0 collective-permute-done.3.from_up
  31.2 0.0 copy-done
  31.2 2.3 %finish.1 = (f32[128,4096]{1,0:T(8,128)}, f32[4,4,8]{2,1,0:T(4,128)}, f32[4,8]{1,0:T(4,128)}) custom-call(f32[128,4096]{1,0:T(8,128)S(1)} %local.1.raw, bf16[128,1024]{1,0:T(8,128)(2,1)S(1)} %collective-permute-done.2.from_down, bf16[128,1024]{1,0:T(8,128)(2,1)S(1)} %collective-permute-done.3.from_up, f32[1,4096]{1,0:T(1,128)S(1)} %bitcast.12, ...), custom_call_target="tpu_custom_call" | custom-call | tf_op jit(solution)/shard_map/finish/pallas_call | solution.py:355
  (3 shorter events, 0.0 us)
Async XLA Ops:
  1.7 13.1 %collective-permute-start.1 = (s32[32,32]{1,0:T(8,128)S(1)}, s32[32,32]{1,0:T(8,128)S(1)}, u32[]{:S(2)}, u32[]{:S(2)}) collective-permute-start(s32[32,32]{1,0:T(8,128)S(1)} %get-tuple-element.19), channel_id=1, source_target_pairs={{0,4},{4,8},{8,12},{12,0},{1,5},{5,9},{9,13},{13,1},{2,6},{6,10},{... | collective-permute-start | bytes 12296 | tf_op jit(solution)/shard_map/ppermute | solution.py:291
  4.8 10.1 %collective-permute-start = (s32[32,32]{1,0:T(8,128)S(1)}, s32[32,32]{1,0:T(8,128)S(1)}, u32[]{:S(2)}, u32[]{:S(2)}) collective-permute-start(s32[32,32]{1,0:T(8,128)S(1)} %get-tuple-element.18), channel_id=1, source_target_pairs={{4,0},{8,4},{12,8},{0,12},{5,1},{9,5},{13,9},{1,13},{6,2},{10,6},{... | collective-permute-start | bytes 12296 | tf_op jit(solution)/shard_map/ppermute | solution.py:290
  11.1 3.7 %collective-permute-start.4 = (f32[8,128]{1,0:T(8,128)S(1)}, f32[8,128]{1,0:T(8,128)S(1)}, u32[]{:S(2)}, u32[]{:S(2)}) collective-permute-start(f32[8,128]{1,0:T(8,128)S(1)} %get-tuple-element.20.totals), channel_id=1, source_target_pairs={{0,2},{2,0},{1,3},{3,1},{4,6},{6,4},{5,7},{7,5},{8,10},{10,8},{9,1... | collective-permute-start | bytes 12296 | tf_op jit(solution)/shard_map/ppermute | solution.py:253
  16.7 14.5 %copy-start = (f32[4096]{0:T(1024)S(1)}, f32[4096]{0:T(1024)}, u32[]{:S(2)}) copy-start(f32[4096]{0:T(1024)} %param.11) | copy-start | bytes 49156
  16.7 14.5 %collective-permute-start.2 = (bf16[128,1024]{1,0:T(8,128)(2,1)S(1)}, bf16[128,1024]{1,0:T(8,128)(2,1)S(1)}, u32[]{:S(2)}, u32[]{:S(2)}) collective-permute-start(bf16[128,1024]{1,0:T(8,128)(2,1)S(1)} %get-tuple-element.21), channel_id=1, source_target_pairs={{0,4},{4,8},{8,12},{12,0},{1,5},{5,9},{9,13},{13,1},{2,6},{6,10},{... | collective-permute-start | bytes 786440 | tf_op jit(solution)/shard_map/ppermute | solution.py:339
  17.2 14.0 %collective-permute-start.3 = (bf16[128,1024]{1,0:T(8,128)(2,1)S(1)}, bf16[128,1024]{1,0:T(8,128)(2,1)S(1)}, u32[]{:S(2)}, u32[]{:S(2)}) collective-permute-start(bf16[128,1024]{1,0:T(8,128)(2,1)S(1)} %get-tuple-element.22), channel_id=1, source_target_pairs={{4,0},{8,4},{12,8},{0,12},{5,1},{9,5},{13,9},{1,13},{6,2},{10,6},{... | collective-permute-start | bytes 786440 | tf_op jit(solution)/shard_map/ppermute | solution.py:340
  20.7 9.8 %collective-permute-start.5 = (f32[8,128]{1,0:T(8,128)S(1)}, f32[8,128]{1,0:T(8,128)S(1)}, u32[]{:S(2)}, u32[]{:S(2)}) collective-permute-start(f32[8,128]{1,0:T(8,128)S(1)} %broadcast_select_fusion), channel_id=1, source_target_pairs={{0,4},{4,0},{8,12},{12,8},{1,5},{5,1},{9,13},{13,9},{2,6},{6,2},{1... | collective-permute-start | bytes 12296 | tf_op jit(solution)/shard_map/ppermute | solution.py:249
  20.7 9.8 %collective-permute-start.6 = (f32[8,128]{1,0:T(8,128)S(1)}, f32[8,128]{1,0:T(8,128)S(1)}, u32[]{:S(2)}, u32[]{:S(2)}) collective-permute-start(f32[8,128]{1,0:T(8,128)S(1)} %broadcast_select_fusion), channel_id=1, source_target_pairs={{0,8},{4,12},{8,0},{12,4},{1,9},{5,13},{9,1},{13,5},{2,10},{6,14},... | collective-permute-start | bytes 12296 | tf_op jit(solution)/shard_map/ppermute | solution.py:249
  21.4 9.7 %collective-permute-start.7 = (f32[8,128]{1,0:T(8,128)S(1)}, f32[8,128]{1,0:T(8,128)S(1)}, u32[]{:S(2)}, u32[]{:S(2)}) collective-permute-start(f32[8,128]{1,0:T(8,128)S(1)} %broadcast_select_fusion), channel_id=1, source_target_pairs={{0,12},{4,8},{8,4},{12,0},{1,13},{5,9},{9,5},{13,1},{2,14},{6,10},... | collective-permute-start | bytes 12296 | tf_op jit(solution)/shard_map/ppermute | solution.py:249

commit v4 on v3

--- a/solution.py
+++ b/solution.py
@@ -12,8 +12,8 @@
 HALO_BLK = 32
 CHUNK = 4
 CHUNK_BITS = 2
-UNROLL = 8
-UNROLL_BITS = 3
+REACH_BITS = 3
+LOCAL_BITS = 4
 PIECES = 8
 PLACE_BITS = 16
 
@@ -143,10 +143,11 @@
     totals[...] = jnp.where(rows == 0, own, rest)
 
 
-def run_items(codes, weighted, tiles, out, work):
+def run_items(codes, weighted, tiles, out, work, bits):
     tile = tiles.shape[1]
     slots = codes.shape[0] - 8
     chunks = slots // CHUNK
+    unroll = 1 << bits
     out[...] = jnp.zeros(out.shape, out.dtype)
 
     def one_target(n, items):
@@ -155,13 +156,13 @@
         return items + ((codes[slots, n] + CHUNK - 1) >> CHUNK_BITS)
 
     count = lax.fori_loop(0, out.shape[1] // tile, one_target, 0)
-    for q in range(UNROLL):
+    for q in range(unroll):
         work[count + q] = (slots + 4) // CHUNK << PLACE_BITS
 
     def one(step, nothing):
         products = []
-        for u in range(UNROLL):
-            item = work[step * UNROLL + u]
+        for u in range(unroll):
+            item = work[step * unroll + u]
             row = (item >> PLACE_BITS) * CHUNK
             column = item & ((1 << PLACE_BITS) - 1)
             left, right = [], []
@@ -177,18 +178,18 @@
                     preferred_element_type=jnp.float32,
                 )
             )
-        for u in range(UNROLL):
-            target = work[step * UNROLL + u] & ((1 << PLACE_BITS) - 1)
+        for u in range(unroll):
+            target = work[step * unroll + u] & ((1 << PLACE_BITS) - 1)
             place = pl.ds(pl.multiple_of(target * tile, tile), tile)
             out[:, place] = out[:, place] + products[u]
         return nothing
 
-    lax.fori_loop(0, (count + UNROLL - 1) >> UNROLL_BITS, one, 0)
+    lax.fori_loop(0, (count + unroll - 1) >> bits, one, 0)
 
 
 def reach_body(codes, weighted, tiles, totals, to_up, to_down, sums, out, work):
     tile = tiles.shape[1]
-    run_items(codes, weighted, tiles, out, work)
+    run_items(codes, weighted, tiles, out, work, REACH_BITS)
     half = to_up.shape[1]
     to_up[...] = out[:, :half].astype(to_up.dtype)
     to_down[...] = out[:, half:].astype(to_down.dtype)
@@ -200,11 +201,12 @@
 
 
 def local_body(codes, weighted, tiles, raw, work):
-    run_items(codes, weighted, tiles, raw, work)
+    run_items(codes, weighted, tiles, raw, work, LOCAL_BITS)
 
 
 def finish_body(
-    raw, from_down, from_up, target, totals, out_hbm, conserved, ensemble, staged, sems
+    raw, from_down, from_up, target, totals, out_hbm, conserved_hbm, ensemble_hbm,
+    staged, conserved, ensemble, sems,
 ):
     columns, cells = raw.shape
     edge = from_down.shape[1]
@@ -213,7 +215,22 @@
     correction = (totals[0:1] - totals[2:3]) / totals[1:2]
     spread = jnp.broadcast_to(correction, (128, columns)).T
     spread = jnp.concatenate([spread] * (piece // 128), axis=1)
-    copies = []
+    members, fields, snapshots = conserved.shape
+    own = totals[0:1] / totals[1:2]
+    every = totals[3:4] / totals[1:2]
+    for f in range(fields):
+        mean = jnp.zeros((1, snapshots), jnp.float32)
+        for m in range(members):
+            begin = (m * fields + f) * snapshots
+            conserved[m, f : f + 1, :] = own[:, begin : begin + snapshots]
+            mean = mean + every[:, begin : begin + snapshots]
+        ensemble[f : f + 1, :] = mean / MEMBERS
+    copies = [
+        pltpu.make_async_copy(conserved, conserved_hbm, sems.at[pieces]),
+        pltpu.make_async_copy(ensemble, ensemble_hbm, sems.at[pieces + 1]),
+    ]
+    for copy in copies:
+        copy.start()
     for n in range(pieces):
         at = pl.ds(n * piece, piece)
         value = raw[:, at]
@@ -224,17 +241,7 @@
             value = value + from_up[:, pl.ds(begin, piece)].astype(jnp.float32)
         staged[:, at] = value / target[:, at] + spread
         copies.append(pltpu.make_async_copy(staged.at[:, at], out_hbm.at[:, at], sems.at[n]))
-        copies[n].start()
-    members, fields, snapshots = conserved.shape
-    own = totals[0:1] / totals[1:2]
-    every = totals[3:4] / totals[1:2]
-    for f in range(fields):
-        mean = jnp.zeros((1, snapshots), jnp.float32)
-        for m in range(members):
-            begin = (m * fields + f) * snapshots
-            conserved[m, f : f + 1, :] = own[:, begin : begin + snapshots]
-            mean = mean + every[:, begin : begin + snapshots]
-        ensemble[f : f + 1, :] = mean / MEMBERS
+        copies[-1].start()
     for copy in copies:
         copy.wait()
 
@@ -360,10 +367,12 @@
             jax.ShapeDtypeStruct((fields, snapshots), f32),
         ),
         in_specs=[VMEM] * 5,
-        out_specs=(ANY, VMEM, VMEM),
+        out_specs=(ANY,) * 3,
         scratch_shapes=[
             pltpu.VMEM((columns, tgt_count * tile), f32),
-            pltpu.SemaphoreType.DMA((piece_count,)),
+            pltpu.VMEM((members, fields, snapshots), f32),
+            pltpu.VMEM((fields, snapshots), f32),
+            pltpu.SemaphoreType.DMA((piece_count + 2,)),
         ],
         compiler_params=params(16),
         name="finish",

time: 33.7 us -> 33.1 us (0.982)
  Pallas kernels: 14.7 us -> 13.7 us
  waiting for transfers between devices: 2.58 us -> 3.05 us
    pallas_call x1, Pallas kernels: 2.28 us -> 1.67 us  [regrid(): pl.pallas_call(finish_body, out_shape=(jax.ShapeDtypeStruct((columns, tgt...]
    ppermute x4, waiting for transfers between devices: 2.57 us -> 3.04 us  [total_over(): lax.ppermute(values, axis, [(i, i ^ step) for i in range(size)])]
    pallas_call x1, Pallas kernels: 5.42 us -> 4.95 us  [regrid(): pl.pallas_call(local_body, out_shape=jax.ShapeDtypeStruct((columns, tgt_c...]
  transfers between devices with their start and end apart: 8 -> 8, of which waited for: 2 -> 3; matrix products, arithmetic and copies ran while one was open for 1% -> 1% of each run, Pallas kernels for 29% -> 28%
where the time goes in v4:
time: 33.1 us; the launch traced here: 32.9 us
  starting transfers between devices  15.2 us (46%)
  Pallas kernels  13.7 us (41%)
  waiting for transfers between devices  3.05 us (9%)
  between operations  0.69 us (2%)
    ppermute x4, starting transfers between devices, total_over(): lax.ppermute(values, axis, [(i, i ^ step) for i in range(size)])  6.1 us
    pallas_call x1, Pallas kernels, regrid(): pl.pallas_call(local_body, out_shape=jax.ShapeDtypeStruct((columns, tgt_c...  4.95 us
    pallas_call x1, Pallas kernels, regrid(): pl.pallas_call(weigh_body, out_shape=(jax.ShapeDtypeStruct((columns, cell...  4.22 us
    ppermute x1, starting transfers between devices, regrid(): from_up = lax.ppermute(to_down, 'band', down)  3.39 us
    ppermute x1, starting transfers between devices, regrid(): down_codes = lax.ppermute(high, 'band', up)  3.1 us
    ppermute x4, waiting for transfers between devices, total_over(): lax.ppermute(values, axis, [(i, i ^ step) for i in range(size)])  3.04 us
    ppermute x1, starting transfers between devices, regrid(): up_codes = lax.ppermute(low, 'band', down)  2.09 us
    pallas_call x1, Pallas kernels, regrid(): pl.pallas_call(reach_body, out_shape=(jax.ShapeDtypeStruct((columns, edge...  1.76 us
  transfers between devices with their start and end apart: 8, of which 3 were waited for; matrix products, arithmetic and copies ran while one was open for 1% of the time, Pallas kernels for 28%

profile of v4, /device:TPU:0, one launch (start us, length us, event | category | flops | bytes accessed | tf_op | source)
XLA Modules:
  0.0 32.9 jit_solution(13219371115310081193)
XLA Ops:
  0.6 1.1 %edges.1 = (s32[32,32]{1,0:T(8,128)S(1)}, s32[32,32]{1,0:T(8,128)S(1)}, s32[32,32]{1,0:T(8,128)S(1)}) custom-call(s32[24,32]{1,0:T(8,128)} %bitcast.17, s32[24,32]{1,0:T(8,128)} %bitcast.18, s32[1,32]{1,0:T(1,128)} %bitcast.19), custom_call_target="tpu_custom_call" | custom-call | tf_op jit(solution)/shard_map/edges/pallas_call | solution.py:283
  1.7 3.1 %collective-permute-start.1 = (s32[32,32]{1,0:T(8,128)S(1)}, s32[32,32]{1,0:T(8,128)S(1)}, u32[]{:S(2)}, u32[]{:S(2)}) collective-permute-start(s32[32,32]{1,0:T(8,128)S(1)} %get-tuple-element.19), channel_id=1, source_target_pairs={{0,4},{4,8},{8,12},{12,0},{1,5},{5,9},{9,13},{13,1},{2,6},{6,10},{... | collective-permute-start | bytes 12296 | tf_op jit(solution)/shard_map/ppermute | solution.py:298
  4.8 2.1 %collective-permute-start = (s32[32,32]{1,0:T(8,128)S(1)}, s32[32,32]{1,0:T(8,128)S(1)}, u32[]{:S(2)}, u32[]{:S(2)}) collective-permute-start(s32[32,32]{1,0:T(8,128)S(1)} %get-tuple-element.18), channel_id=1, source_target_pairs={{4,0},{8,4},{12,8},{0,12},{5,1},{9,5},{13,9},{1,13},{6,2},{10,6},{... | collective-permute-start | bytes 12296 | tf_op jit(solution)/shard_map/ppermute | solution.py:297
  6.9 4.2 %weigh.1 = (bf16[128,16384]{1,0:T(8,128)(2,1)S(1)}, f32[8,128]{1,0:T(8,128)S(1)}, bf16[17,128,128]{2,1,0:T(8,128)(2,1)S(1)}) custom-call(bf16[128,16384]{1,0:T(8,128)(2,1)} %bitcast.13, s32[1,16384]{1,0:T(1,128)} %bitcast.14, f32[1,16384]{1,0:T(1,128)} %bitcast.15, f32[1,4096]{1,0:T(1,128)} %bitcast.11, bf16[16,128,128]{2,1,0:T(8,128)(2,1)} %tiles_hbm.1, ...), custom_call_target="tpu_custom_call" | custom-call | tf_op jit(solution)/shard_map/weigh/pallas_call | solution.py:300
  11.1 1.7 %collective-permute-start.4 = (f32[8,128]{1,0:T(8,128)S(1)}, f32[8,128]{1,0:T(8,128)S(1)}, u32[]{:S(2)}, u32[]{:S(2)}) collective-permute-start(f32[8,128]{1,0:T(8,128)S(1)} %get-tuple-element.20.totals), channel_id=1, source_target_pairs={{0,2},{2,0},{1,3},{3,1},{4,6},{6,4},{5,7},{7,5},{8,10},{10,8},{9,1... | collective-permute-start | bytes 12296 | tf_op jit(solution)/shard_map/ppermute | solution.py:260
  12.8 2.0 %collective-permute-done.4 = f32[8,128]{1,0:T(8,128)S(1)} collective-permute-done((f32[8,128]{1,0:T(8,128)S(1)}, f32[8,128]{1,0:T(8,128)S(1)}, u32[]{:S(2)}, u32[]{:S(2)}) %collective-permute-start.4) | collective-permute-done | bytes 4128 | tf_op jit(solution)/shard_map/ppermute | solution.py:260
  14.8 0.0 collective-permute-done.1
  14.8 0.1 slice.13
  14.9 0.0 collective-permute-done
  14.9 0.1 pad_add_fusion.codes
  15.0 1.8 %reach.1 = (bf16[128,1024]{1,0:T(8,128)(2,1)S(1)}, bf16[128,1024]{1,0:T(8,128)(2,1)S(1)}, f32[8,128]{1,0:T(8,128)S(1)}) custom-call(s32[32,16]{1,0:T(8,128)S(1)} %pad_add_fusion.codes, bf16[128,16384]{1,0:T(8,128)(2,1)S(1)} %get-tuple-element.16.weighted, bf16[17,128,128]{2,1,0:T(8,128)(2,1)S(1)} %get-tuple-element.17.tiles, ...), custom_call_target="tpu_custom_call" | custom-call | tf_op jit(solution)/shard_map/reach/pallas_call | solution.py:330
  16.7 0.0 copy-start
  16.7 0.5 %collective-permute-start.2 = (bf16[128,1024]{1,0:T(8,128)(2,1)S(1)}, bf16[128,1024]{1,0:T(8,128)(2,1)S(1)}, u32[]{:S(2)}, u32[]{:S(2)}) collective-permute-start(bf16[128,1024]{1,0:T(8,128)(2,1)S(1)} %get-tuple-element.21), channel_id=1, source_target_pairs={{0,4},{4,8},{8,12},{12,0},{1,5},{5,9},{9,13},{13,1},{2,6},{6,10},{... | collective-permute-start | bytes 786440 | tf_op jit(solution)/shard_map/ppermute | solution.py:346
  17.2 3.4 %collective-permute-start.3 = (bf16[128,1024]{1,0:T(8,128)(2,1)S(1)}, bf16[128,1024]{1,0:T(8,128)(2,1)S(1)}, u32[]{:S(2)}, u32[]{:S(2)}) collective-permute-start(bf16[128,1024]{1,0:T(8,128)(2,1)S(1)} %get-tuple-element.22), channel_id=1, source_target_pairs={{4,0},{8,4},{12,8},{0,12},{5,1},{9,5},{13,9},{1,13},{6,2},{10,6},{... | collective-permute-start | bytes 786440 | tf_op jit(solution)/shard_map/ppermute | solution.py:347
  20.6 0.1 broadcast_select_fusion
  20.7 0.0 collective-permute-start.5
  20.7 0.7 %collective-permute-start.6 = (f32[8,128]{1,0:T(8,128)S(1)}, f32[8,128]{1,0:T(8,128)S(1)}, u32[]{:S(2)}, u32[]{:S(2)}) collective-permute-start(f32[8,128]{1,0:T(8,128)S(1)} %broadcast_select_fusion), channel_id=1, source_target_pairs={{0,8},{4,12},{8,0},{12,4},{1,9},{5,13},{9,1},{13,5},{2,10},{6,14},... | collective-permute-start | bytes 12296 | tf_op jit(solution)/shard_map/ppermute | solution.py:256
  21.4 3.7 %collective-permute-start.7 = (f32[8,128]{1,0:T(8,128)S(1)}, f32[8,128]{1,0:T(8,128)S(1)}, u32[]{:S(2)}, u32[]{:S(2)}) collective-permute-start(f32[8,128]{1,0:T(8,128)S(1)} %broadcast_select_fusion), channel_id=1, source_target_pairs={{0,12},{4,8},{8,4},{12,0},{1,13},{5,9},{9,5},{13,1},{2,14},{6,10},... | collective-permute-start | bytes 12296 | tf_op jit(solution)/shard_map/ppermute | solution.py:256
  25.1 5.0 %local.1.raw = f32[128,4096]{1,0:T(8,128)S(1)} custom-call(s32[32,32]{1,0:T(8,128)S(1)} %get-tuple-element.15.codes, bf16[128,16384]{1,0:T(8,128)(2,1)S(1)} %get-tuple-element.16.weighted, bf16[17,128,128]{2,1,0:T(8,128)(2,1)S(1)} %get-tuple-element.17.tiles), custom_call_target="tpu_custom_call" | custom-call | tf_op jit(solution)/shard_map/local/pallas_call | solution.py:351
  30.0 0.0 collective-permute-done.5
  30.0 0.1 collective-permute-done.6
  30.2 1.0 %collective-permute-done.7 = f32[8,128]{1,0:T(8,128)S(1)} collective-permute-done((f32[8,128]{1,0:T(8,128)S(1)}, f32[8,128]{1,0:T(8,128)S(1)}, u32[]{:S(2)}, u32[]{:S(2)}) %collective-permute-start.7) | collective-permute-done | bytes 4128 | tf_op jit(solution)/shard_map/ppermute | solution.py:256
  31.1 0.1 add_add_fusion.totals
  31.2 0.0 collective-permute-done.2.from_down
  31.2 0.0 collective-permute-done.3.from_up
  31.2 0.0 copy-done
  31.2 1.7 %finish.1 = (f32[128,4096]{1,0:T(8,128)}, f32[4,4,8]{2,1,0:T(4,128)}, f32[4,8]{1,0:T(4,128)}) custom-call(f32[128,4096]{1,0:T(8,128)S(1)} %local.1.raw, bf16[128,1024]{1,0:T(8,128)(2,1)S(1)} %collective-permute-done.2.from_down, bf16[128,1024]{1,0:T(8,128)(2,1)S(1)} %collective-permute-done.3.from_up, f32[1,4096]{1,0:T(1,128)S(1)} %bitcast.12, ...), custom_call_target="tpu_custom_call" | custom-call | tf_op jit(solution)/shard_map/finish/pallas_call | solution.py:362
  (3 shorter events, 0.0 us)
Async XLA Ops:
  1.7 13.1 %collective-permute-start.1 = (s32[32,32]{1,0:T(8,128)S(1)}, s32[32,32]{1,0:T(8,128)S(1)}, u32[]{:S(2)}, u32[]{:S(2)}) collective-permute-start(s32[32,32]{1,0:T(8,128)S(1)} %get-tuple-element.19), channel_id=1, source_target_pairs={{0,4},{4,8},{8,12},{12,0},{1,5},{5,9},{9,13},{13,1},{2,6},{6,10},{... | collective-permute-start | bytes 12296 | tf_op jit(solution)/shard_map/ppermute | solution.py:298
  4.8 10.1 %collective-permute-start = (s32[32,32]{1,0:T(8,128)S(1)}, s32[32,32]{1,0:T(8,128)S(1)}, u32[]{:S(2)}, u32[]{:S(2)}) collective-permute-start(s32[32,32]{1,0:T(8,128)S(1)} %get-tuple-element.18), channel_id=1, source_target_pairs={{4,0},{8,4},{12,8},{0,12},{5,1},{9,5},{13,9},{1,13},{6,2},{10,6},{... | collective-permute-start | bytes 12296 | tf_op jit(solution)/shard_map/ppermute | solution.py:297
  11.1 3.7 %collective-permute-start.4 = (f32[8,128]{1,0:T(8,128)S(1)}, f32[8,128]{1,0:T(8,128)S(1)}, u32[]{:S(2)}, u32[]{:S(2)}) collective-permute-start(f32[8,128]{1,0:T(8,128)S(1)} %get-tuple-element.20.totals), channel_id=1, source_target_pairs={{0,2},{2,0},{1,3},{3,1},{4,6},{6,4},{5,7},{7,5},{8,10},{10,8},{9,1... | collective-permute-start | bytes 12296 | tf_op jit(solution)/shard_map/ppermute | solution.py:260
  16.7 14.5 %copy-start = (f32[4096]{0:T(1024)S(1)}, f32[4096]{0:T(1024)}, u32[]{:S(2)}) copy-start(f32[4096]{0:T(1024)} %param.11) | copy-start | bytes 49156
  16.7 14.5 %collective-permute-start.2 = (bf16[128,1024]{1,0:T(8,128)(2,1)S(1)}, bf16[128,1024]{1,0:T(8,128)(2,1)S(1)}, u32[]{:S(2)}, u32[]{:S(2)}) collective-permute-start(bf16[128,1024]{1,0:T(8,128)(2,1)S(1)} %get-tuple-element.21), channel_id=1, source_target_pairs={{0,4},{4,8},{8,12},{12,0},{1,5},{5,9},{9,13},{13,1},{2,6},{6,10},{... | collective-permute-start | bytes 786440 | tf_op jit(solution)/shard_map/ppermute | solution.py:346
  17.2 14.0 %collective-permute-start.3 = (bf16[128,1024]{1,0:T(8,128)(2,1)S(1)}, bf16[128,1024]{1,0:T(8,128)(2,1)S(1)}, u32[]{:S(2)}, u32[]{:S(2)}) collective-permute-start(bf16[128,1024]{1,0:T(8,128)(2,1)S(1)} %get-tuple-element.22), channel_id=1, source_target_pairs={{4,0},{8,4},{12,8},{0,12},{5,1},{9,5},{13,9},{1,13},{6,2},{10,6},{... | collective-permute-start | bytes 786440 | tf_op jit(solution)/shard_map/ppermute | solution.py:347
  20.7 9.3 %collective-permute-start.5 = (f32[8,128]{1,0:T(8,128)S(1)}, f32[8,128]{1,0:T(8,128)S(1)}, u32[]{:S(2)}, u32[]{:S(2)}) collective-permute-start(f32[8,128]{1,0:T(8,128)S(1)} %broadcast_select_fusion), channel_id=1, source_target_pairs={{0,4},{4,0},{8,12},{12,8},{1,5},{5,1},{9,13},{13,9},{2,6},{6,2},{1... | collective-permute-start | bytes 12296 | tf_op jit(solution)/shard_map/ppermute | solution.py:256
  20.7 9.5 %collective-permute-start.6 = (f32[8,128]{1,0:T(8,128)S(1)}, f32[8,128]{1,0:T(8,128)S(1)}, u32[]{:S(2)}, u32[]{:S(2)}) collective-permute-start(f32[8,128]{1,0:T(8,128)S(1)} %broadcast_select_fusion), channel_id=1, source_target_pairs={{0,8},{4,12},{8,0},{12,4},{1,9},{5,13},{9,1},{13,5},{2,10},{6,14},... | collective-permute-start | bytes 12296 | tf_op jit(solution)/shard_map/ppermute | solution.py:256
  21.4 9.7 %collective-permute-start.7 = (f32[8,128]{1,0:T(8,128)S(1)}, f32[8,128]{1,0:T(8,128)S(1)}, u32[]{:S(2)}, u32[]{:S(2)}) collective-permute-start(f32[8,128]{1,0:T(8,128)S(1)} %broadcast_select_fusion), channel_id=1, source_target_pairs={{0,12},{4,8},{8,4},{12,0},{1,13},{5,9},{9,5},{13,1},{2,14},{6,10},... | collective-permute-start | bytes 12296 | tf_op jit(solution)/shard_map/ppermute | solution.py:256
